TPU v7x, 128 devices: a whole 4x4x4 slice. The times are simulated.
128 devices in a mesh: blocks: 64 (over x, z, y), cross: 2 (over core).
Axes of the slice: x: 4, y: 4, z: 4, core: 2. Of those that a mesh axis runs over, the one named last changes fastest.
Arguments:
- f_home: float32 [4096, 19, 512], P(('blocks', 'cross')), may hold values from -0.5 to 1.5
- levels: int32 [4096], P(('blocks', 'cross')), may hold values from 0 to 1, as said below
- plan: int32 [4096], P(('blocks', 'cross')), may hold values from 0 to 4095, as said below
Outputs:
- f_owner: float32 [4096, 19, 512], P(('blocks', 'cross'))
Inputs may be any that keep to these rules, and one draw needn't show every extreme that they name: `levels`: exactly a quarter of the patches, 8 times the number of devices, have level 1. plan is a permutation of the patch numbers. Of the patches in the slots of one device of f_home, at most 2 have owner slots on one device, and in every draw some device sends exactly 2 to one owner; every device's owner slots receive exactly 8 patches of level 1.
All inputs are finite; a program needn't handle non-finite values.
Results may differ from a plain program's by a relative error of at most 0.0001.
Values sent between devices are 32-bit elements; how exact they have to be, the bound alone decides.
A program may use at most 256 MiB of HBM per device.

v0:
```python
import jax
import jax.numpy as jnp
from jax import lax
from jax.sharding import PartitionSpec as P

FLOW_PATCHES = 1
SPAN_PATCHES = 4
DEPTH_PATCHES = 8
EDGE = 8
STEPS = 2
CELLS = 512


VELOCITIES = (
    (0, 0, 0),
    (1, 0, 0),
    (-1, 0, 0),
    (0, 1, 0),
    (0, -1, 0),
    (0, 0, 1),
    (0, 0, -1),
    (1, 1, 0),
    (-1, -1, 0),
    (1, -1, 0),
    (-1, 1, 0),
    (1, 0, 1),
    (-1, 0, -1),
    (1, 0, -1),
    (-1, 0, 1),
    (0, 1, 1),
    (0, -1, -1),
    (0, 1, -1),
    (0, -1, 1),
)
WEIGHTS = (1.0 / 3.0,) + (1.0 / 18.0,) * 6 + (1.0 / 36.0,) * 12
FACE_SPEEDS = (
    (2, 8, 10, 12, 14),
    (1, 7, 9, 11, 13),
    (4, 8, 9, 16, 18),
    (3, 7, 10, 15, 17),
    (6, 12, 13, 16, 17),
    (5, 11, 14, 15, 18),
)
TAU_COARSE = 0.55
TAU_FINE = 2.0 * TAU_COARSE - 0.5
RESCALE = TAU_FINE / (2.0 * TAU_COARSE)
INFLOW = 0.08


def extended_2(cells, sides, width):
    for axis, dim in sides:
        count = lax.axis_size(axis)
        head = lax.slice_in_dim(cells, 0, width, axis=dim)
        tail = lax.slice_in_dim(cells, cells.shape[dim] - width, cells.shape[dim], axis=dim)
        cells = jnp.concatenate(
            [
                lax.ppermute(tail, axis, [(i, (i + 1) % count) for i in range(count)]),
                cells,
                lax.ppermute(head, axis, [((i + 1) % count, i) for i in range(count)]),
            ],
            axis=dim,
        )
    return cells


def moments(field):
    density = jnp.sum(field, axis=1)
    velocity = []
    for axis_id in range(3):
        forward = [speed for speed in range(19) if VELOCITIES[speed][axis_id] == 1]
        backward = [speed for speed in range(19) if VELOCITIES[speed][axis_id] == -1]
        velocity.append(
            (jnp.sum(field[:, forward], axis=1) - jnp.sum(field[:, backward], axis=1)) / density
        )
    return (density, velocity)


def equilibrium(density, velocity, speeds):
    speed_sq = velocity[0] * velocity[0] + velocity[1] * velocity[1] + velocity[2] * velocity[2]
    columns = []
    for speed in speeds:
        step_x, step_y, step_z = VELOCITIES[speed]
        along = step_x * velocity[0] + step_y * velocity[1] + step_z * velocity[2]
        columns.append(
            WEIGHTS[speed] * density * (1.0 + 3.0 * along + 4.5 * along * along - 1.5 * speed_sq)
        )
    return jnp.stack(columns, axis=1)


def collide(field, relax_rate):
    density, velocity = moments(field)
    balance = equilibrium(density, velocity, range(19))
    relaxed = field + relax_rate[:, None, None, None, None] * (balance - field)
    return (relaxed, balance, density, velocity)


def layer(field, face_id):
    picker = [slice(None)] * field.ndim
    picker[2 + face_id // 2] = 0 if face_id % 2 == 0 else field.shape[-1] - 1
    return field[tuple(picker)]


def face_payload(relaxed, balance, send_scale):
    eq_faces = jnp.stack(
        [layer(balance[:, list(FACE_SPEEDS[face_id])], face_id) for face_id in range(6)], axis=1
    )
    out_faces = jnp.stack(
        [layer(relaxed[:, list(FACE_SPEEDS[face_id])], face_id) for face_id in range(6)], axis=1
    )
    return (eq_faces, send_scale[:, None, None, None, None] * (out_faces - eq_faces))


def inflow_column(speeds):
    values = []
    for speed in speeds:
        along = VELOCITIES[speed][0] * INFLOW
        values.append(
            WEIGHTS[speed] * (1.0 + 3.0 * along + 4.5 * along * along - 1.5 * INFLOW * INFLOW)
        )
    return jnp.array(values, jnp.float32)


def framed(center, top_row, bottom_row, left_col, right_col):
    middle = jnp.concatenate([left_col[..., :, None], center, right_col[..., :, None]], axis=-1)
    corner = jnp.zeros(top_row.shape[:-1] + (1,), top_row.dtype)
    upper = jnp.concatenate([corner, top_row, corner], axis=-1)[..., None, :]
    lower = jnp.concatenate([corner, bottom_row, corner], axis=-1)[..., None, :]
    return jnp.concatenate([upper, middle, lower], axis=-2)


def bordered(center, left_col, right_col):
    return jnp.concatenate([left_col[..., None], center, right_col[..., None]], axis=-1)


def assemble(eq_ext, neq_ext, recv_scale, inflow_side, outflow_side):
    size_x, size_y, size_z = recv_scale.shape
    factor = recv_scale[:, :, :, None, None, None]

    def neighbour(shift_x, shift_y, shift_z, face_id):
        window = (
            slice(1 + shift_x, 1 + shift_x + size_x),
            slice(1 + shift_y, 1 + shift_y + size_y),
            slice(1 + shift_z, 1 + shift_z + size_z),
            face_id,
        )
        return eq_ext[window] + factor * neq_ext[window]

    plane_west = framed(
        neighbour(-1, 0, 0, 1),
        neighbour(-1, -1, 0, 1)[..., -1, :],
        neighbour(-1, 1, 0, 1)[..., 0, :],
        neighbour(-1, 0, -1, 1)[..., :, -1],
        neighbour(-1, 0, 1, 1)[..., :, 0],
    )
    plane_east = framed(
        neighbour(1, 0, 0, 0),
        neighbour(1, -1, 0, 0)[..., -1, :],
        neighbour(1, 1, 0, 0)[..., 0, :],
        neighbour(1, 0, -1, 0)[..., :, -1],
        neighbour(1, 0, 1, 0)[..., :, 0],
    )
    plane_south = bordered(
        neighbour(0, -1, 0, 3),
        neighbour(0, -1, -1, 3)[..., :, -1],
        neighbour(0, -1, 1, 3)[..., :, 0],
    )
    plane_north = bordered(
        neighbour(0, 1, 0, 2), neighbour(0, 1, -1, 2)[..., :, -1], neighbour(0, 1, 1, 2)[..., :, 0]
    )
    plane_below = neighbour(0, 0, -1, 5)
    plane_above = neighbour(0, 0, 1, 4)
    plane_west = jnp.where(
        inflow_side[:, None, None, None, None, None],
        inflow_column(FACE_SPEEDS[1])[:, None, None],
        plane_west,
    )
    plane_east = jnp.where(
        outflow_side[:, None, None, None, None, None],
        inflow_column(FACE_SPEEDS[0])[:, None, None],
        plane_east,
    )
    return (plane_west, plane_east, plane_south, plane_north, plane_below, plane_above)


def propagate(relaxed, planes):
    extent = relaxed.shape[-1]
    padded = jnp.pad(relaxed, ((0, 0), (0, 0), (1, 1), (1, 1), (1, 1)))
    plane_west, plane_east, plane_south, plane_north, plane_below, plane_above = planes
    for column, speed in enumerate(FACE_SPEEDS[1]):
        padded = padded.at[:, speed, 0, :, :].set(plane_west[:, column])
    for column, speed in enumerate(FACE_SPEEDS[0]):
        padded = padded.at[:, speed, extent + 1, :, :].set(plane_east[:, column])
    for column, speed in enumerate(FACE_SPEEDS[3]):
        padded = padded.at[:, speed, 1 : extent + 1, 0, :].set(plane_south[:, column])
    for column, speed in enumerate(FACE_SPEEDS[2]):
        padded = padded.at[:, speed, 1 : extent + 1, extent + 1, :].set(plane_north[:, column])
    for column, speed in enumerate(FACE_SPEEDS[5]):
        padded = padded.at[:, speed, 1 : extent + 1, 1 : extent + 1, 0].set(plane_below[:, column])
    for column, speed in enumerate(FACE_SPEEDS[4]):
        padded = padded.at[:, speed, 1 : extent + 1, 1 : extent + 1, extent + 1].set(
            plane_above[:, column]
        )
    shifted = []
    for speed in range(19):
        step_x, step_y, step_z = VELOCITIES[speed]
        shifted.append(
            padded[
                :,
                speed,
                1 - step_x : 1 - step_x + extent,
                1 - step_y : 1 - step_y + extent,
                1 - step_z : 1 - step_z + extent,
            ]
        )
    return jnp.stack(shifted, axis=1)


def wrap_axis(values, axis_id):
    length = values.shape[axis_id]
    return jnp.concatenate(
        [
            lax.slice_in_dim(values, length - 1, length, axis=axis_id),
            values,
            lax.slice_in_dim(values, 0, 1, axis=axis_id),
        ],
        axis=axis_id,
    )


def pair_slots(target_dev):
    patch_total = target_dev.shape[0]
    order = jnp.arange(patch_total, dtype=jnp.int32)
    earlier = (target_dev[:, None] == target_dev[None, :]) & (order[None, :] < order[:, None])
    return jnp.sum(earlier.astype(jnp.int32), axis=1)


def pack(payload, target_dev, pair_slot, devices, capacity):
    buffer = jnp.zeros((devices, capacity) + payload.shape[1:], payload.dtype)
    return buffer.at[target_dev, pair_slot].set(payload)


def migrate(populations, levels, plan, target_dev, pair_slot, devices, capacity):
    patch_total = populations.shape[0]
    metadata = jnp.stack([plan % patch_total + 1, levels], axis=1)
    recv_state, recv_meta = (
        lax.all_to_all(
            pack(populations, target_dev, pair_slot, devices, capacity),
            ("blocks", "cross"),
            split_axis=0,
            concat_axis=0,
            tiled=True,
        ),
        lax.all_to_all(
            pack(metadata, target_dev, pair_slot, devices, capacity),
            ("blocks", "cross"),
            split_axis=0,
            concat_axis=0,
            tiled=True,
        ),
    )
    total = devices * capacity
    flat_meta = recv_meta.reshape(total, 2)
    target = jnp.where(flat_meta[:, 0] > 0, flat_meta[:, 0] - 1, patch_total)
    anchor = jnp.arange(total, dtype=jnp.int32)
    moved = (
        jnp.zeros(populations.shape, populations.dtype)
        .at[target]
        .set(recv_state.reshape((total,) + populations.shape[1:]), mode="drop")
    )
    owner_levels = jnp.zeros((patch_total,), jnp.int32).at[target].set(flat_meta[:, 1], mode="drop")
    source_dev = (
        jnp.zeros((patch_total,), jnp.int32).at[target].set(anchor // capacity, mode="drop")
    )
    source_pair = (
        jnp.zeros((patch_total,), jnp.int32).at[target].set(anchor % capacity, mode="drop")
    )
    return (moved, owner_levels, source_dev, source_pair)


def home_ghosts(eq_faces, neq_faces, home_levels):
    lattice_shape = (FLOW_PATCHES, SPAN_PATCHES, DEPTH_PATCHES)
    patch_total = eq_faces.shape[0]
    stacked = jnp.stack([eq_faces, neq_faces], axis=1).reshape(lattice_shape + (-1,))
    extended = extended_2(stacked, (("blocks", 0), ("cross", 1)), 1)
    extended = wrap_axis(extended, 2)
    extended = extended.reshape(extended.shape[:3] + (2, 6, 5, EDGE, EDGE))
    recv_scale = (
        jnp.where(home_levels == 1, RESCALE, 1.0).astype(jnp.float32).reshape(lattice_shape)
    )
    span_x = FLOW_PATCHES * lax.axis_size("blocks")
    position = lax.axis_index("blocks") * FLOW_PATCHES + jnp.arange(FLOW_PATCHES, dtype=jnp.int32)
    planes = assemble(
        extended[:, :, :, 0],
        extended[:, :, :, 1],
        recv_scale,
        position == 0,
        position == span_x - 1,
    )
    return tuple((plane.reshape((patch_total,) + plane.shape[3:]) for plane in planes))


def body(f_home, levels, plan):
    devices = lax.axis_size(("blocks", "cross"))
    patch_total = f_home.shape[0]
    capacity = (patch_total + devices - 1) // devices + 1
    target_dev = plan // patch_total
    pair_slot = pair_slots(target_dev)
    send_home = jnp.where(levels == 1, 1.0 / RESCALE, 1.0).astype(jnp.float32)
    cube = (patch_total, 19, EDGE, EDGE, EDGE)
    populations = f_home.reshape(cube)
    fine_mask = levels == 1
    relax_rate = jnp.where(fine_mask, 1.0 / TAU_FINE, 1.0 / TAU_COARSE).astype(jnp.float32)
    fine_rate = jnp.full((patch_total,), 1.0 / TAU_FINE, jnp.float32)
    for round_id in range(STEPS):
        relaxed, balance, density, velocity = collide(populations, relax_rate)
        eq_faces, neq_faces = face_payload(relaxed, balance, send_home)
        planes = home_ghosts(eq_faces, neq_faces, levels)
        populations = propagate(relaxed, planes)
        updated = propagate(collide(populations, fine_rate)[0], planes)
        populations = jnp.where(fine_mask[:, None, None, None, None], updated, populations)
    return migrate(
        populations.reshape(patch_total, 19, CELLS),
        levels,
        plan,
        target_dev,
        pair_slot,
        devices,
        capacity,
    )[0]


def solution(mesh):
    in_specs = (P(("blocks", "cross"), None, None), P(("blocks", "cross")), P(("blocks", "cross")))
    out_specs = P(("blocks", "cross"), None, None)
    return jax.shard_map(body, mesh=mesh, in_specs=in_specs, out_specs=out_specs, check_vma=False)
```

profile of v0, /device:TPU:1, one launch (start us, length us, event | category | flops | bytes accessed | tf_op | source)
XLA Modules:
  0.0 1282.9 jit_solution(9917443473619058868)
XLA Ops:
  65.4 8.0 multiply_add_fusion.3
  117.1 7.4 collective-permute-start.1
  124.5 10.6 collective-permute-done
  136.6 10.2 pad.493
  151.7 27.5 %reshape.8613 = f32[3,6,10,2,6,5,8,8]{7,6,5,4,3,1,2,0:T(8,128)} reshape(f32[3,6,10,3840]{3,1,2,0:T(8,128)} %copy.787) | data formatting | bytes 5529600 | tf_op jit(solution)/shard_map/reshape | solution.py:286
  179.2 22.4 %slice_bitcast_fusion = (f32[3,6,10,6,5,8,8]{6,5,4,3,1,2,0:T(8,128)}, f32[3,6,10,1,6,5,8,8]{7,6,5,4,3,1,2,0:T(8,128)S(1)}) fusion(f32[3,6,10,2,6,5,8,8]{7,6,5,4,3,1,2,0:T(8,128)} %reshape.8613), kind=kLoop, calls=%fused_computation.51 | loop fusion | bytes 5529600 | tf_op jit(solution)/shard_map/squeeze | solution.py:294
  201.6 8.3 copy.1034
  209.9 8.3 fusion.344
  243.6 9.4 fusion.343
  279.2 6.4 slice_add_fusion.9
  423.8 7.7 pad.494
  482.0 5.9 fusion.339
  562.3 8.0 multiply_add_fusion.1
  611.3 7.2 collective-permute-start.5
  618.5 11.1 collective-permute-done.4
  635.5 9.0 all-to-all-start
  644.5 10.2 pad.495
  657.5 27.9 %reshape.9083 = f32[3,6,10,2,6,5,8,8]{7,6,5,4,3,2,1,0:T(8,128)} reshape(f32[3,6,10,3840]{3,2,1,0:T(8,128)} %fusion) | data formatting | bytes 5529600 | tf_op jit(solution)/shard_map/reshape | solution.py:286
  685.3 22.5 %fusion.340 = (f32[3,6,10,1,6,5,8,8]{7,6,5,4,3,2,1,0:T(8,128)}, f32[3,6,10,1,6,5,8,8]{7,6,5,4,3,2,1,0:T(8,128)S(1)}) fusion(f32[3,6,10,2,6,5,8,8]{7,6,5,4,3,2,1,0:T(8,128)} %reshape.9083), kind=kLoop, calls=%fused_computation.991 | loop fusion | bytes 5529600 | tf_op jit(solution)/shard_map/slice | solution.py:294
  707.8 7.9 copy.1033
  715.7 8.3 fusion.342
  727.8 17.2 %copy.1032 = f32[3,6,10,1,6,5,8,8]{7,6,5,1,2,4,0,3:T(8,128)} copy(f32[3,6,10,1,6,5,8,8]{7,6,5,4,3,2,1,0:T(8,128)} %get-tuple-element.1465) | data formatting | bytes 2764800
  745.0 9.3 fusion.341
  801.9 6.8 slice_add_fusion.1
  868.9 5.8 fusion.345
  982.4 7.7 pad.496
  1079.7 6.2 broadcast_in_dim.269
  1091.5 18.2 %copy.982 = f32[128,2,19,512]{3,1,2,0:T(2,128)} copy(f32[128,2,19,512]{3,2,1,0:T(8,128)} %scatter_fusion.1) | data formatting | bytes 19922944 | tf_op jit(solution)/shard_map/scatter | solution.py:239
  1109.7 10.1 all-to-all-start.1
  1120.8 122.9 %all-to-all-done.1 = f32[128,2,19,512]{3,1,2,0:T(2,128)} async-done(((f32[128,2,19,512]{3,1,2,0:T(2,128)}), f32[128,2,19,512]{3,1,2,0:T(2,128)}, u32[]{:S(2)}, u32[]{:S(2)}) %all-to-all-start.1) | async-done | bytes 9961504 | tf_op jit(solution)/shard_map/all_to_all | solution.py:246
  1243.7 11.2 copy.990
  1255.1 25.6 %scatter_fusion.2 = f32[32,19,512]{2,1,0:T(8,128)S(1)} fusion(f32[32,19,512]{2,1,0:T(8,128)S(1)} %broadcast_in_dim.265, s32[256]{0:T(256)S(1)} %bitcast.1274, f32[256,19,512]{2,1,0:T(8,128)} %bitcast.1156), kind=kCustom, calls=%fused_computation.50 | custom fusion | bytes 29885440 | tf_op jit(solution)/shard_map/scatter | solution.py:268
  (881 shorter events, 794.3 us)
Async XLA Ops:
  4.4 565.9 %copy-start.105 = (s32[1024]{0:T(1024)}, s32[1024]{0:T(1024)S(1)}, u32[]{:S(2)}) copy-start(s32[1024]{0:T(1024)S(1)} %get-tuple-element.1650) | copy-start | bytes 12292
  10.9 70.7 %copy-start.106 = (s32[1024]{0:T(1024)}, s32[1024]{0:T(1024)S(1)}, u32[]{:S(2)}) copy-start(s32[1024]{0:T(1024)S(1)} %get-tuple-element.1648) | copy-start | bytes 12292
  10.9 74.8 %copy-start.108 = (s32[1024]{0:T(1024)}, s32[1024]{0:T(1024)S(1)}, u32[]{:S(2)}) copy-start(s32[1024]{0:T(1024)S(1)} %get-tuple-element.1649) | copy-start | bytes 12292
  17.3 71.4 %copy-start.110 = (s32[1024]{0:T(1024)}, s32[1024]{0:T(1024)S(1)}, u32[]{:S(2)}) copy-start(s32[1024]{0:T(1024)S(1)} %get-tuple-element.1646) | copy-start | bytes 12292
  17.4 74.5 %copy-start.111 = (s32[1024]{0:T(1024)}, s32[1024]{0:T(1024)S(1)}, u32[]{:S(2)}) copy-start(s32[1024]{0:T(1024)S(1)} %get-tuple-element.1647) | copy-start | bytes 12292
  65.4 38.3 %copy-start.113 = (f32[32]{0:T(128)}, f32[32]{0:T(128)S(1)}, u32[]{:S(2)}) copy-start(f32[32]{0:T(128)S(1)} %get-tuple-element.1643) | copy-start | bytes 388
  65.4 81.4 %copy-start.112 = (f32[32]{0:T(128)}, f32[32]{0:T(128)S(1)}, u32[]{:S(2)}) copy-start(f32[32]{0:T(128)S(1)} %get-tuple-element.1641) | copy-start | bytes 388
  114.9 20.2 %collective-permute-start = (f32[1,4,8,3840]{3,2,1,0:T(8,128)S(1)}, f32[1,4,8,3840]{3,2,1,0:T(8,128)S(1)}, u32[]{:S(2)}, u32[]{:S(2)}) collective-permute-start(f32[1,4,8,3840]{3,2,1,0:T(8,128)S(1)} %copy.986), channel_id=1, source_target_pairs={{0,2},{2,4},{4,6},{6,8},{8,10},{10,12},{12,14},{14,16},{16,18},{18... | collective-permute-start | bytes 1474568 | tf_op jit(solution)/shard_map/ppermute | solution.py:57
  117.1 18.0 %collective-permute-start.1 = (f32[1,4,8,3840]{3,2,1,0:T(8,128)S(1)}, f32[1,4,8,3840]{3,2,1,0:T(8,128)S(1)}, u32[]{:S(2)}, u32[]{:S(2)}) collective-permute-start(f32[1,4,8,3840]{3,2,1,0:T(8,128)S(1)} %copy.986), channel_id=1, source_target_pairs={{2,0},{4,2},{6,4},{8,6},{10,8},{12,10},{14,12},{16,14},{18,16},{20... | collective-permute-start | bytes 1474568 | tf_op jit(solution)/shard_map/ppermute | solution.py:59
  135.2 12.3 collective-permute-start.2
  136.5 11.0 collective-permute-start.3
  147.0 155.4 %copy-start.87 = (f32[4,8]{0,1:T(8,128)}, f32[4,8]{0,1:T(8,128)S(1)}, u32[]{:S(2)}) copy-start(f32[4,8]{0,1:T(8,128)S(1)} %copy.789) | copy-start | bytes 388
  327.9 47.6 %copy-start.73 = (f32[32,1,8,8]{0,3,2,1:T(8,128)}, f32[32,1,8,8]{0,3,2,1:T(8,128)S(1)}, u32[]{:S(2)}) copy-start(f32[32,1,8,8]{0,3,2,1:T(8,128)S(1)} %get-tuple-element.1600) | copy-start | bytes 24580
  327.9 47.6 %copy-start.77 = (f32[32,1,8,8]{0,3,2,1:T(8,128)}, f32[32,1,8,8]{0,3,2,1:T(8,128)S(1)}, u32[]{:S(2)}) copy-start(f32[32,1,8,8]{0,3,2,1:T(8,128)S(1)} %get-tuple-element.1601) | copy-start | bytes 24580
  327.9 47.6 %copy-start.79 = (f32[32,1,8,8]{0,3,2,1:T(8,128)}, f32[32,1,8,8]{0,3,2,1:T(8,128)S(1)}, u32[]{:S(2)}) copy-start(f32[32,1,8,8]{0,3,2,1:T(8,128)S(1)} %get-tuple-element.1602) | copy-start | bytes 24580
  327.9 47.6 %copy-start.81 = (f32[32,1,8,8]{0,3,2,1:T(8,128)}, f32[32,1,8,8]{0,3,2,1:T(8,128)S(1)}, u32[]{:S(2)}) copy-start(f32[32,1,8,8]{0,3,2,1:T(8,128)S(1)} %get-tuple-element.1603) | copy-start | bytes 24580
  327.9 47.6 %copy-start.83 = (f32[32,1,8,8]{0,3,2,1:T(8,128)}, f32[32,1,8,8]{0,3,2,1:T(8,128)S(1)}, u32[]{:S(2)}) copy-start(f32[32,1,8,8]{0,3,2,1:T(8,128)S(1)} %get-tuple-element.1604) | copy-start | bytes 24580
  328.0 49.4 %copy-start.71 = (f32[32,1,8,8]{0,3,2,1:T(8,128)}, f32[32,1,8,8]{0,3,2,1:T(8,128)S(1)}, u32[]{:S(2)}) copy-start(f32[32,1,8,8]{0,3,2,1:T(8,128)S(1)} %get-tuple-element.1598) | copy-start | bytes 24580
  328.0 49.4 %copy-start.75 = (f32[32,1,8,8]{0,3,2,1:T(8,128)}, f32[32,1,8,8]{0,3,2,1:T(8,128)S(1)}, u32[]{:S(2)}) copy-start(f32[32,1,8,8]{0,3,2,1:T(8,128)S(1)} %get-tuple-element.1599) | copy-start | bytes 24580
  423.8 27.6 %copy-start.74 = (f32[32,1,8,8]{0,3,2,1:T(8,128)S(1)}, f32[32,1,8,8]{0,3,2,1:T(8,128)}, u32[]{:S(2)}) copy-start(f32[32,1,8,8]{0,3,2,1:T(8,128)} %copy-done.73) | copy-start | bytes 24580
  423.8 29.3 %copy-start.76 = (f32[32,1,8,8]{0,3,2,1:T(8,128)S(1)}, f32[32,1,8,8]{0,3,2,1:T(8,128)}, u32[]{:S(2)}) copy-start(f32[32,1,8,8]{0,3,2,1:T(8,128)} %copy-done.75) | copy-start | bytes 24580
  423.8 31.1 %copy-start.72 = (f32[32,1,8,8]{0,3,2,1:T(8,128)S(1)}, f32[32,1,8,8]{0,3,2,1:T(8,128)}, u32[]{:S(2)}) copy-start(f32[32,1,8,8]{0,3,2,1:T(8,128)} %copy-done.71) | copy-start | bytes 24580
  611.2 18.4 %collective-permute-start.4 = (f32[1,4,8,3840]{3,2,1,0:T(8,128)S(1)}, f32[1,4,8,3840]{3,2,1,0:T(8,128)S(1)}, u32[]{:S(2)}, u32[]{:S(2)}) collective-permute-start(f32[1,4,8,3840]{3,2,1,0:T(8,128)S(1)} %copy.987), channel_id=1, source_target_pairs={{0,2},{2,4},{4,6},{6,8},{8,10},{10,12},{12,14},{14,16},{16,18},{18... | collective-permute-start | bytes 1474568 | tf_op jit(solution)/shard_map/ppermute | solution.py:57
  611.3 18.4 %collective-permute-start.5 = (f32[1,4,8,3840]{3,2,1,0:T(8,128)S(1)}, f32[1,4,8,3840]{3,2,1,0:T(8,128)S(1)}, u32[]{:S(2)}, u32[]{:S(2)}) collective-permute-start(f32[1,4,8,3840]{3,2,1,0:T(8,128)S(1)} %copy.987), channel_id=1, source_target_pairs={{2,0},{4,2},{6,4},{8,6},{10,8},{12,10},{14,12},{16,14},{18,16},{20... | collective-permute-start | bytes 1474568 | tf_op jit(solution)/shard_map/ppermute | solution.py:59
  629.7 25.0 %collective-permute-start.6 = (f32[3,1,8,3840]{3,2,1,0:T(8,128)S(1)}, f32[3,1,8,3840]{3,2,1,0:T(8,128)S(1)}, u32[]{:S(2)}, u32[]{:S(2)}) collective-permute-start(f32[3,1,8,3840]{3,2,1,0:T(8,128)S(1)} %get-tuple-element.1581), channel_id=1, source_target_pairs={{0,1},{1,0},{2,3},{3,2},{4,5},{5,4},{6,7},{7,6},{8,9},{9,8},{10,11... | collective-permute-start | bytes 1105928 | tf_op jit(solution)/shard_map/ppermute | solution.py:57
  630.7 24.0 %collective-permute-start.7 = (f32[3,1,8,3840]{3,2,1,0:T(8,128)S(1)}, f32[3,1,8,3840]{3,2,1,0:T(8,128)S(1)}, u32[]{:S(2)}, u32[]{:S(2)}) collective-permute-start(f32[3,1,8,3840]{3,2,1,0:T(8,128)S(1)} %get-tuple-element.1582), channel_id=1, source_target_pairs={{1,0},{0,1},{3,2},{2,3},{5,4},{4,5},{7,6},{6,7},{9,8},{8,9},{11,10... | collective-permute-start | bytes 1105928 | tf_op jit(solution)/shard_map/ppermute | solution.py:59
  635.5 474.2 %all-to-all-start = ((s32[128,2,2]{2,1,0:T(2,128)}), s32[128,2,2]{2,1,0:T(2,128)}, u32[]{:S(2)}, u32[]{:S(2)}) async-start(s32[128,2,2]{2,1,0:T(2,128)} %scatter_fusion), calls=%async_computation | async-start | bytes 262144 | tf_op jit(solution)/shard_map/all_to_all | solution.py:253
  982.4 27.6 %copy-start.60 = (f32[32,1,8,8]{0,3,2,1:T(8,128)S(1)}, f32[32,1,8,8]{0,3,2,1:T(8,128)}, u32[]{:S(2)}) copy-start(f32[32,1,8,8]{0,3,2,1:T(8,128)} %copy-done.59) | copy-start | bytes 24580
  982.4 29.3 %copy-start.62 = (f32[32,1,8,8]{0,3,2,1:T(8,128)S(1)}, f32[32,1,8,8]{0,3,2,1:T(8,128)}, u32[]{:S(2)}) copy-start(f32[32,1,8,8]{0,3,2,1:T(8,128)} %copy-done.61) | copy-start | bytes 24580
  982.4 31.1 %copy-start.58 = (f32[32,1,8,8]{0,3,2,1:T(8,128)S(1)}, f32[32,1,8,8]{0,3,2,1:T(8,128)}, u32[]{:S(2)}) copy-start(f32[32,1,8,8]{0,3,2,1:T(8,128)} %copy-done.57) | copy-start | bytes 24580
  1031.0 47.6 %copy-start.118 = (pred[32]{0:T(512)(128)(4,1)S(1)}, pred[32]{0:T(512)(128)(4,1)}, u32[]{:S(2)}) copy-start(pred[32]{0:T(512)(128)(4,1)} %broadcast_compare_fusion) | copy-start | bytes 100
  1109.7 134.0 %all-to-all-start.1 = ((f32[128,2,19,512]{3,1,2,0:T(2,128)}), f32[128,2,19,512]{3,1,2,0:T(2,128)}, u32[]{:S(2)}, u32[]{:S(2)}) async-start(f32[128,2,19,512]{3,1,2,0:T(2,128)} %copy.982), calls=%async_computation.1 | async-start | bytes 19922944 | tf_op jit(solution)/shard_map/all_to_all | solution.py:246
  (106 other events, 1563.9 us)
where the time goes:
time: 1310 us; the launch traced here: 1280 us
  local copies, waits for them, and re-layouts  959 us (73%)
  waiting for transfers between devices  145 us (11%)
  other arithmetic  137 us (10%)
  starting transfers between devices  38.6 us (3%)
    unnamed x379, local copies, waits for them, and re-layouts  151 us
    all_to_all x1, waiting for transfers between devices, migrate(): lax.all_to_all(pack(populations, target_dev, pair_slot, devices, capacity...  123 us
    slice x28, local copies, waits for them, and re-layouts, neighbour(): return eq_ext[window] + factor * neq_ext[window]  90 us
    another operation x43, local copies, waits for them, and re-layouts, propagate(): return jnp.stack(shifted, axis=1)  62.5 us
    gather x23, local copies, waits for them, and re-layouts, face_payload(): balance[:, list(FACE_SPEEDS[face_id])]  55.4 us
    reshape x2, local copies, waits for them, and re-layouts, home_ghosts(): extended = extended.reshape(extended.shape[:3] + (2, 6, 5, EDGE, EDGE))  55.4 us
    squeeze x24, local copies, waits for them, and re-layouts, neighbour(): return eq_ext[window] + factor * neq_ext[window]  48.1 us
    unnamed x72, other arithmetic  47.8 us
  transfers between devices with their start and end apart: 10, of which 3 were waited for; matrix products, arithmetic and copies ran while one was open for 37% of the time, Pallas kernels for 0%

commit v1 on v0

v1 whole, which is shorter than its diff:
```python
import jax
import jax.numpy as jnp
from jax import lax
from jax.experimental import pallas as pl
from jax.experimental.pallas import tpu as pltpu
from jax.sharding import PartitionSpec as P

STEPS = 2
MESH = pl.DeviceIdType.MESH
VELOCITIES = (
    (0, 0, 0),
    (1, 0, 0),
    (-1, 0, 0),
    (0, 1, 0),
    (0, -1, 0),
    (0, 0, 1),
    (0, 0, -1),
    (1, 1, 0),
    (-1, -1, 0),
    (1, -1, 0),
    (-1, 1, 0),
    (1, 0, 1),
    (-1, 0, -1),
    (1, 0, -1),
    (-1, 0, 1),
    (0, 1, 1),
    (0, -1, -1),
    (0, 1, -1),
    (0, -1, 1),
)
WEIGHTS = (1.0 / 3.0,) + (1.0 / 18.0,) * 6 + (1.0 / 36.0,) * 12
PAIRS = tuple((q, q + 1) for q in range(1, 19, 2))
X_SPEEDS = ((1, 7, 9, 11, 13), (2, 8, 10, 12, 14))
Y_SPEEDS = ((3, 7, 10, 15, 17), (4, 8, 9, 16, 18))
TAU_COARSE = 0.55
TAU_FINE = 2.0 * TAU_COARSE - 0.5
RESCALE = TAU_FINE / (2.0 * TAU_COARSE)
INFLOW = 0.08
ROWS = 76


def inflow_value(speed):
    along = VELOCITIES[speed][0] * INFLOW
    return WEIGHTS[speed] * (1.0 + 3.0 * along + 4.5 * along * along - 1.5 * INFLOW * INFLOW)


def equilibrium(field):
    density = field[0]
    for q in range(1, 19):
        density = density + field[q]
    inverse = 1.0 / density
    velocity = []
    for axis in range(3):
        total = None
        for q in range(1, 19):
            sign = VELOCITIES[q][axis]
            if sign:
                if total is None:
                    total = field[q] if sign > 0 else -field[q]
                else:
                    total = total + field[q] if sign > 0 else total - field[q]
        velocity.append(total * inverse)
    ux, uy, uz = velocity
    base = 1.0 - 1.5 * (ux * ux + uy * uy + uz * uz)
    out = [None] * 19
    out[0] = WEIGHTS[0] * density * base
    for plus, minus in PAIRS:
        along = None
        for axis in range(3):
            sign = VELOCITIES[plus][axis]
            if sign:
                term = velocity[axis]
                if along is None:
                    along = term
                else:
                    along = along + term if sign > 0 else along - term
        even = base + 4.5 * along * along
        odd = 3.0 * along
        scale = WEIGHTS[plus] * density
        out[plus] = scale * (even + odd)
        out[minus] = scale * (even - odd)
    return out


def lattice_masks(shape):
    lane = lax.broadcasted_iota(jnp.int32, shape, len(shape) - 1)
    return lane, (lane // 8) % 8, lane % 8


def wide_roll(values, shift, axis):
    shift = shift % values.shape[axis]
    return values if shift == 0 else pltpu.roll(values, shift, axis)


def shifted(main, before, after, q):
    ex, ey, ez = VELOCITIES[q]
    lane, j, k = lattice_masks((1, 8, 128))
    if ex > 0:
        other = jnp.concatenate([before[None], main[:3]], axis=0)
        main = jnp.where(lane[None] < 64, main, other)
    elif ex < 0:
        other = jnp.concatenate([main[1:], after[None]], axis=0)
        main = jnp.where(lane[None] >= 64, main, other)
    turn = 64 if ex else 0
    here = main[:, 1:5].reshape(16, 8, 128)
    if ey > 0:
        there = main[:, 0:4].reshape(16, 8, 128)
        here = jnp.where(j > 0, wide_roll(here, turn + 8, 2), wide_roll(there, turn - 56, 2))
        turn = 0
    elif ey < 0:
        there = main[:, 2:6].reshape(16, 8, 128)
        here = jnp.where(j < 7, wide_roll(here, turn - 8, 2), wide_roll(there, turn + 56, 2))
        turn = 0
    if ez > 0:
        over = wide_roll(wide_roll(here, 1, 1), turn - 7, 2)
        here = jnp.where(k > 0, wide_roll(here, turn + 1, 2), over)
    elif ez < 0:
        over = wide_roll(wide_roll(here, 7, 1), turn + 7, 2)
        here = jnp.where(k < 7, wide_roll(here, turn - 1, 2), over)
    else:
        here = wide_roll(here, turn, 2)
    return here


def shifted_inside(main, q):
    ex, ey, ez = VELOCITIES[q]
    shape = (4, 1, 8, 128)
    lane, j, k = lattice_masks(shape)
    high = lax.broadcasted_iota(jnp.int32, shape, 0)
    inside = lane >= 0
    if ex > 0:
        other = jnp.concatenate([main[:1], main[:3]], axis=0)
        main = jnp.where(lane < 64, main, other)
        inside = inside & (high * 128 + lane >= 64)
    elif ex < 0:
        other = jnp.concatenate([main[1:], main[3:]], axis=0)
        main = jnp.where(lane >= 64, main, other)
        inside = inside & (high * 128 + lane < 448)
    if ey:
        inside = inside & ((j > 0) if ey > 0 else (j < 7))
    if ez:
        inside = inside & ((k > 0) if ez > 0 else (k < 7))
    turn = (64 if ex else 0) + 8 * ey + ez
    moved = wide_roll(main.reshape(16, 8, 128), turn, 2)
    return moved.reshape(4, 4, 8, 128), inside


def lbm_kernel(blocks, f_hbm, levels, x_out, raw, state, both, work, pack_x, halo_x, coef, load_sem, send_sem, recv_sem):
    b = lax.axis_index("blocks")
    c = lax.axis_index("cross")
    has_low, has_high = b > 0, b < blocks - 1
    low, high = jnp.maximum(b - 1, 0), jnp.minimum(b + 1, blocks - 1)

    for ih in range(4):
        pltpu.make_async_copy(
            f_hbm.at[:, :, pl.ds(128 * ih, 128)], raw.at[ih, :, pl.ds(0, 19)], load_sem.at[ih]
        ).start()

    barrier = pltpu.get_barrier_semaphore()

    def greet(device):
        pl.semaphore_signal(barrier, inc=1, device_id=device, device_id_type=MESH)

    greet((b, 1 - c))

    @pl.when(has_low)
    def _():
        greet((low, c))
        greet((low, 1 - c))

    @pl.when(has_high)
    def _():
        greet((high, c))
        greet((high, 1 - c))

    sublane = lax.broadcasted_iota(jnp.int32, (8, 128), 0)
    for py in range(4):
        fine = jnp.zeros((8, 128), jnp.float32)
        for pz in range(8):
            fine = jnp.where(sublane == pz, levels[py * 8 + pz].astype(jnp.float32), fine)
        is_fine = fine > 0.5
        coef[0, py] = fine
        coef[1, py] = jnp.where(is_fine, (1.0 - 1.0 / TAU_FINE) / RESCALE, 1.0 - 1.0 / TAU_COARSE)
        coef[2, py] = jnp.where(is_fine, 1.0 - 1.0 / TAU_FINE, RESCALE * (1.0 - 1.0 / TAU_COARSE))

    for step in range(STEPS):
        for side in range(2):

            @pl.when(jnp.logical_not(has_low if side == 0 else has_high))
            def _():
                for n, q in enumerate(X_SPEEDS[side]):
                    halo_x[step, side, n] = jnp.full((6, 8, 128), inflow_value(q), jnp.float32)

    for ih in range(4):
        pltpu.make_async_copy(
            f_hbm.at[:, :, pl.ds(128 * ih, 128)], raw.at[ih, :, pl.ds(0, 19)], load_sem.at[ih]
        ).wait()
    pl.semaphore_wait(
        barrier, 1 + 2 * has_low.astype(jnp.int32) + 2 * has_high.astype(jnp.int32)
    )

    lane = lax.broadcasted_iota(jnp.int32, (4, 8, 128), 2)
    pending = []
    for step in range(STEPS):

        def relax_both(pos, carry):
            ih, py = pos // 4, pos % 4
            rows = pl.ds(pl.multiple_of(py * 8, 8), 8)
            if step:
                field = [state[q, ih, rows, :] for q in range(19)]
            else:
                flat = raw.at[ih].reshape(768, 128)
                field = [flat[pl.ds(py * 192 + q, 8, stride=24), :] for q in range(19)]
            balance = equilibrium(field)
            for_coarse, for_fine = coef[1, py], coef[2, py]
            for q in range(19):
                away = field[q] - balance[q]
                both[step, 0, q, ih, py + 1] = balance[q] + for_coarse * away
                both[step, 1, q, ih, py + 1] = balance[q] + for_fine * away
            return carry

        lax.fori_loop(0, 16, relax_both, 0)

        copies = []

        def add(src, dst, device, send_if, recv_if):
            index = len(copies)
            copy = pltpu.make_async_remote_copy(
                src_ref=src,
                dst_ref=dst,
                send_sem=send_sem.at[step, index],
                recv_sem=recv_sem.at[step, index],
                device_id=device,
                device_id_type=MESH,
            )
            copies.append((send_if, recv_if, copy))

        for side in range(2):
            edge = 3 if side == 0 else 0
            for n, q in enumerate(X_SPEEDS[side]):
                first = both[step, 0, q, edge, 1:5]
                second = pltpu.roll(both[step, 1, q, edge, 1:5], 64, 2)
                keep = lane >= 64 if side == 0 else lane < 64
                pack_x[step, side, n] = jnp.where(keep, first, second)
        for side in range(2):
            target = high if side == 0 else low
            send_if, recv_if = (has_high, has_low) if side == 0 else (has_low, has_high)
            add(
                pack_x.at[step, side],
                halo_x.at[step, side, :, pl.ds(1, 4)],
                (target, c),
                send_if,
                recv_if,
            )
            for n, q in enumerate(X_SPEEDS[side]):
                ey = VELOCITIES[q][1]
                if ey:
                    py, slot = (3, 0) if ey > 0 else (0, 5)
                    add(
                        pack_x.at[step, side, n, py],
                        halo_x.at[step, side, n, slot],
                        (target, 1 - c),
                        send_if,
                        recv_if,
                    )
        for side in range(2):
            py, slot = (4, 0) if side == 0 else (1, 5)
            for q in Y_SPEEDS[side]:
                add(
                    both.at[step, :, q, :, py],
                    both.at[step, :, q, :, slot],
                    (b, 1 - c),
                    None,
                    None,
                )
        for send_if, recv_if, copy in copies:
            if send_if is None:
                copy.start()
            else:
                pl.when(send_if)(copy.start)
        for send_if, recv_if, copy in copies:
            if recv_if is None:
                copy.wait_recv()
            else:
                pl.when(recv_if)(copy.wait_recv)
        pending += copies

        fine = coef[0] > 0.5
        for q in range(19):
            ex = VELOCITIES[q][0]
            result = []
            for kind in range(2):
                before = after = None
                if ex > 0:
                    before = halo_x[step, 0, X_SPEEDS[0].index(q)]
                    before = pltpu.roll(before, 64, 2) if kind else before
                elif ex < 0:
                    after = halo_x[step, 1, X_SPEEDS[1].index(q)]
                    after = pltpu.roll(after, 64, 2) if kind else after
                main = both[step, kind, q]
                result.append(shifted(main, before, after, q).reshape(4, 4, 8, 128))
            state[q] = jnp.where(fine[None], result[1], result[0]).reshape(4, 32, 128)

        def relax_again(pos, carry):
            ih, py = pos // 4, pos % 4
            rows = pl.ds(pl.multiple_of(py * 8, 8), 8)
            field = [state[q, ih, rows, :] for q in range(19)]
            balance = equilibrium(field)
            for q in range(19):
                work[q, ih, py] = field[q] + (1.0 / TAU_FINE) * (balance[q] - field[q])
            return carry

        lax.fori_loop(0, 16, relax_again, 0)
        for q in range(19):
            moved, inside = shifted_inside(work[q], q)
            kept = state[q].reshape(4, 4, 8, 128)
            result = jnp.where(inside & fine[None], moved, kept).reshape(4, 32, 128)
            if step == STEPS - 1:
                x_out[pl.ds(4 * q, 4)] = result
            else:
                state[q] = result

    for send_if, recv_if, copy in pending:
        if send_if is None:
            copy.wait_send()
        else:
            pl.when(send_if)(copy.wait_send)


def row_holder(row):
    spare = row - 64
    x, e = spare // 3, spare % 3
    chip = 16 * x + 4 * ((e + x) % 4) + (e + 3 * x) % 4
    return jnp.where(row < 64, row, chip), jnp.where(row < 64, 1, 0)


def row_of(b, c):
    x, z, y = b // 16, (b // 4) % 4, b % 4
    e = (z + 4 - x) % 4
    spare = (e < 3) & (y == (e + 3 * x) % 4)
    row = jnp.where(c == 1, b, 64 + 3 * x + e)
    return row, (c == 1) | spare


def migrate_kernel(
    devices, x_ref, plan_ref, out_ref, plan_all, plan_turned, inv_vec, inv_smem, gathered, ordered,
    local_sem, plan_send, plan_recv, spread_send, spread_recv, home_send, home_recv,
):
    b = lax.axis_index("blocks")
    c = lax.axis_index("cross")
    me = 2 * b + c
    my_row, is_mid = row_of(b, c)
    barrier = pltpu.get_barrier_semaphore()

    def each_other(body):
        def step(k, carry):
            other = (me + k) % devices
            body(other, (other // 2, other % 2))
            return carry

        lax.fori_loop(1, devices, step, 0)

    each_other(
        lambda other, device: pl.semaphore_signal(
            barrier, inc=1, device_id=device, device_id_type=MESH
        )
    )
    plan_all[me] = plan_ref[...]
    pl.semaphore_wait(barrier, devices - 1)

    def send_plan(other, device):
        pltpu.make_async_remote_copy(
            src_ref=plan_ref,
            dst_ref=plan_all.at[me],
            send_sem=plan_send,
            recv_sem=plan_recv,
            device_id=device,
            device_id_type=MESH,
        ).start()

    each_other(send_plan)

    def send_row(k, carry):
        row = (my_row + 1 + k) % ROWS
        device = row_holder(row)

        @pl.when((device[0] != b) | (device[1] != c))
        def _():
            pltpu.make_async_remote_copy(
                src_ref=x_ref.at[row],
                dst_ref=gathered.at[pl.ds(pl.multiple_of(me * 32, 32), 32)],
                send_sem=spread_send,
                recv_sem=spread_recv,
                device_id=device,
                device_id_type=MESH,
            ).start()

        return carry

    lax.fori_loop(0, ROWS, send_row, 0)

    def wait_for(sem, blocks_of_rows):
        part = gathered.at[pl.ds(0, 32 * blocks_of_rows)]
        pltpu.make_async_copy(part, part, sem).wait()

    others = plan_all.at[pl.ds(0, devices - 1)]
    pltpu.make_async_copy(others, others, plan_recv).wait()

    @pl.when(is_mid)
    def _():
        gathered[pl.ds(pl.multiple_of(me * 32, 32), 32), :] = x_ref[my_row]
        plans = plan_all[:, 0, :]
        plan_turned[...] = plans.T
        sub = lax.broadcasted_iota(jnp.int32, (128, 128), 0)
        lane = lax.broadcasted_iota(jnp.int32, (128, 128), 1)

        def place(p, carry):
            plans, total = carry
            owner = plan_turned[pl.ds(p, 1), :] // 32
            hot = jnp.where(owner == sub, 1.0, 0.0)
            slot = plans[:, 0:1] % 32
            value = jnp.where(slot == lane, sub, jnp.where(slot + 32 == lane, p, 0))
            total = total + jnp.dot(
                hot.astype(jnp.bfloat16),
                value.astype(jnp.float32).astype(jnp.bfloat16),
                preferred_element_type=jnp.float32,
            )
            return pltpu.roll(plans, 127, 1), total

        _, total = lax.fori_loop(0, 32, place, (plans, jnp.zeros((128, 128), jnp.float32)))
        total = total.astype(jnp.int32)
        inv_vec[...] = jnp.clip(total * 32 + pltpu.roll(total, 96, 1), 0, 32 * devices - 1)
        move = pltpu.make_async_copy(inv_vec, inv_smem, local_sem)
        move.start()
        move.wait()
        wait_for(spread_recv, devices - 1)

        def place_at(owner):
            return ordered.at[pl.ds(pl.multiple_of(owner * 32, 32), 32)]

        def target():
            return out_ref.at[my_row]

        def send_owner(owner):
            pltpu.make_async_remote_copy(
                src_ref=place_at(owner),
                dst_ref=target(),
                send_sem=home_send,
                recv_sem=home_recv,
                device_id=(owner // 2, owner % 2),
                device_id_type=MESH,
            ).start()

        def pick(k, carry):
            owner = (me + k) % devices
            for u in range(32):
                index = inv_smem[owner, u]
                ordered[pl.ds(owner * 32 + u, 1), :] = gathered[pl.ds(index, 1), :]

            @pl.when(k > 1)
            def _():
                send_owner((me + k - 1) % devices)

            return carry

        lax.fori_loop(1, devices + 1, pick, 0)
        out_ref[my_row] = ordered[pl.ds(pl.multiple_of(me * 32, 32), 32), :]
        wait_for(home_send, devices - 1)
        wait_for(spread_send, ROWS - 1)
        wait_for(home_recv, ROWS - 1)

    @pl.when(jnp.logical_not(is_mid))
    def _():
        wait_for(spread_send, ROWS)
        wait_for(home_recv, ROWS)

    pltpu.make_async_copy(others, others, plan_send).wait()


def lbm_call(f_home, levels):
    blocks = lax.axis_size("blocks")
    vmem = pl.BlockSpec(memory_space=pltpu.VMEM)
    return pl.pallas_call(
        lambda *refs: lbm_kernel(blocks, *refs),
        out_shape=jax.ShapeDtypeStruct((ROWS, 32, 128), jnp.float32),
        in_specs=[pl.BlockSpec(memory_space=pl.ANY), pl.BlockSpec(memory_space=pltpu.SMEM)],
        out_specs=vmem,
        scratch_shapes=[
            pltpu.VMEM((4, 32, 24, 128), jnp.float32),
            pltpu.VMEM((19, 4, 32, 128), jnp.float32),
            pltpu.VMEM((STEPS, 2, 19, 4, 6, 8, 128), jnp.float32),
            pltpu.VMEM((19, 4, 4, 8, 128), jnp.float32),
            pltpu.VMEM((STEPS, 2, 5, 4, 8, 128), jnp.float32),
            pltpu.VMEM((STEPS, 2, 5, 6, 8, 128), jnp.float32),
            pltpu.VMEM((3, 4, 8, 128), jnp.float32),
            pltpu.SemaphoreType.DMA((4,)),
            pltpu.SemaphoreType.DMA((STEPS, 16)),
            pltpu.SemaphoreType.DMA((STEPS, 16)),
        ],
        compiler_params=pltpu.CompilerParams(
            collective_id=0, has_side_effects=True, vmem_limit_bytes=60 * 1024 * 1024
        ),
        name="lbm",
    )(f_home, levels)


def body(f_home, levels, plan):
    blocks = lax.axis_size("blocks")
    devices = 2 * blocks
    vmem = pl.BlockSpec(memory_space=pltpu.VMEM)
    state = lbm_call(f_home, levels)
    rows = pl.pallas_call(
        lambda *refs: migrate_kernel(devices, *refs),
        out_shape=jax.ShapeDtypeStruct((ROWS, 32, 128), jnp.float32),
        in_specs=[vmem, vmem],
        out_specs=vmem,
        scratch_shapes=[
            pltpu.VMEM((devices, 1, 128), jnp.int32),
            pltpu.VMEM((128, 128), jnp.int32),
            pltpu.VMEM((128, 128), jnp.int32),
            pltpu.SMEM((128, 128), jnp.int32),
            pltpu.VMEM((devices * 32, 128), jnp.float32),
            pltpu.VMEM((devices * 32, 128), jnp.float32),
        ]
        + [pltpu.SemaphoreType.DMA] * 7,
        compiler_params=pltpu.CompilerParams(
            collective_id=1, has_side_effects=True, vmem_limit_bytes=60 * 1024 * 1024
        ),
        name="migrate",
    )(state, jnp.pad(plan, (0, 96)).reshape(1, 128))
    return rows.reshape(19, 4, 32, 128).transpose(2, 0, 1, 3).reshape(32, 19, 512)


def solution(mesh):
    spec = P(("blocks", "cross"))
    return jax.shard_map(
        body, mesh=mesh, in_specs=(spec, spec, spec), out_specs=spec, check_vma=False
    )
```

time: 1310 us -> 104 us (0.08)
  the two profiles are of different devices: /device:TPU:1 before, /device:TPU:101 now
where the time goes in v1:
time: 104 us
  Pallas kernels  97.7 us (94%)
  local copies, waits for them, and re-layouts  6.19 us (6%)
    pallas_call x1, Pallas kernels, body(): pl.pallas_call(lambda *refs: migrate_kernel(devices, *refs), out_shape=ja...  72.5 us
    pallas_call x1, Pallas kernels, lbm_call(): pl.pallas_call(lambda *refs: lbm_kernel(blocks, *refs), out_shape=jax.Sha...  25.2 us
    unnamed x3, local copies, waits for them, and re-layouts  3.19 us
    reshape x1, local copies, waits for them, and re-layouts, body(): rows.reshape(19, 4, 32, 128).transpose(2, 0, 1, 3).reshape(32, 19, 512)  2.49 us

profile of v1, /device:TPU:101, one launch (start us, length us, event | category | flops | bytes accessed | tf_op | source)
XLA Modules:
  0.0 103.9 jit_solution(15755474857983709315)
XLA Ops:
  0.0 3.2 %copy.4.refs_0_ = f32[32,19,512]{2,1,0:T(8,128)} copy(f32[32,19,512]{2,0,1:T(8,128)} %param.3) | data formatting | bytes 2490368 | tf_op args[0]
  3.2 0.0 copy-start
  3.2 25.2 %lbm.1.refs_0_ = f32[76,32,128]{2,1,0:T(8,128)} custom-call(f32[32,19,512]{2,1,0:T(8,128)} %copy.4.refs_0_, s32[32]{0:T(128)} %refs_1_.1), custom_call_target="tpu_custom_call" | custom-call | tf_op jit(solution)/shard_map/lbm/pallas_call | solution.py:483
  28.4 0.0 copy-done
  28.4 0.5 pad_bitcast_fusion.refs_1_
  28.9 72.5 %migrate.1 = f32[76,32,128]{2,1,0:T(8,128)} custom-call(f32[76,32,128]{2,1,0:T(8,128)} %lbm.1.refs_0_, s32[1,128]{1,0:T(1,128)} %pad_bitcast_fusion.refs_1_), custom_call_target="tpu_custom_call" | custom-call | tf_op jit(solution)/shard_map/migrate/pallas_call | solution.py:512
  101.4 2.5 %copy.8 = f32[19,4,4,8,128]{4,3,1,2,0:T(8,128)} copy(f32[19,4,4,8,128]{4,3,2,1,0:T(8,128)} %bitcast.9) | data formatting | bytes 2490368 | tf_op jit(solution)/shard_map/reshape | solution.py:531
Async XLA Ops:
  3.2 25.2 %copy-start = (s32[32]{0:T(128)S(1)}, s32[32]{0:T(128)}, u32[]{:S(2)}) copy-start(s32[32]{0:T(128)} %param.5) | copy-start | bytes 388

commit v2 on v1

--- a/solution.py
+++ b/solution.py
@@ -37,6 +37,8 @@
 RESCALE = TAU_FINE / (2.0 * TAU_COARSE)
 INFLOW = 0.08
 ROWS = 76
+UNITS = 48
+VMEM_LIMIT = 28 * 1024 * 1024
 
 
 def inflow_value(speed):
@@ -145,16 +147,27 @@
     return moved.reshape(4, 4, 8, 128), inside
 
 
-def lbm_kernel(blocks, f_hbm, levels, x_out, raw, state, both, work, pack_x, halo_x, coef, load_sem, send_sem, recv_sem):
+def lbm_steps(
+    blocks, f_hbm, levels_hbm, plan_hbm, rows, plan_all, levels, plan, raw, state, both, work, pack_x, halo_x, coef,
+    load_sem, send_sem, recv_sem, round_send, round_recv,
+):
     b = lax.axis_index("blocks")
     c = lax.axis_index("cross")
     has_low, has_high = b > 0, b < blocks - 1
     low, high = jnp.maximum(b - 1, 0), jnp.minimum(b + 1, blocks - 1)
 
-    for ih in range(4):
+    loads = [
         pltpu.make_async_copy(
-            f_hbm.at[:, :, pl.ds(128 * ih, 128)], raw.at[ih, :, pl.ds(0, 19)], load_sem.at[ih]
-        ).start()
+            f_hbm.at[:, :, pl.ds(128 * ih, 128)], raw.at[ih], load_sem.at[ih]
+        )
+        for ih in range(4)
+    ]
+    numbers = [
+        pltpu.make_async_copy(levels_hbm, levels, load_sem.at[4]),
+        pltpu.make_async_copy(plan_hbm, plan, load_sem.at[5]),
+    ]
+    for load in numbers + loads:
+        load.start()
 
     barrier = pltpu.get_barrier_semaphore()
 
@@ -173,6 +186,8 @@
         greet((high, c))
         greet((high, 1 - c))
 
+    for load in numbers:
+        load.wait()
     sublane = lax.broadcasted_iota(jnp.int32, (8, 128), 0)
     for py in range(4):
         fine = jnp.zeros((8, 128), jnp.float32)
@@ -191,13 +206,50 @@
                 for n, q in enumerate(X_SPEEDS[side]):
                     halo_x[step, side, n] = jnp.full((6, 8, 128), inflow_value(q), jnp.float32)
 
-    for ih in range(4):
-        pltpu.make_async_copy(
-            f_hbm.at[:, :, pl.ds(128 * ih, 128)], raw.at[ih, :, pl.ds(0, 19)], load_sem.at[ih]
-        ).wait()
+    plan_row = jnp.zeros((1, 128), jnp.int32)
+    plan_lane = lax.broadcasted_iota(jnp.int32, (1, 128), 1)
+    for p in range(32):
+        plan_row = jnp.where(plan_lane == p, plan[p], plan_row)
+    plan_all[64 * c + b] = plan_row
+
+    def line(axis):
+        stride = (16, 4, 1)[axis]
+        at = (b // stride) % 4
+        return [b + stride * ((at + k) % 4 - at) for k in (1, 2, 3)]
+
+    for axis in range(3):
+        for chip in line(axis):
+            greet((chip, c))
+
+    def plan_round(number):
+        size = (1, 4, 16, 64)[number]
+        part = plan_all.at[pl.ds(64 * c + (b // size) * size, size)]
+        peers = [(b, 1 - c)] if number == 3 else [(chip, c) for chip in line(2 - number)]
+        copies = [
+            pltpu.make_async_remote_copy(
+                src_ref=part,
+                dst_ref=part,
+                send_sem=round_send.at[number],
+                recv_sem=round_recv.at[number],
+                device_id=peer,
+                device_id_type=MESH,
+            )
+            for peer in peers
+        ]
+        for copy in copies:
+            copy.start()
+
+    def end_round(number):
+        moved = plan_all.at[pl.ds(0, (3, 12, 48, 64)[number])]
+        pltpu.make_async_copy(moved, moved, round_recv.at[number]).wait()
+        pltpu.make_async_copy(moved, moved, round_send.at[number]).wait()
+
+    for load in loads:
+        load.wait()
     pl.semaphore_wait(
-        barrier, 1 + 2 * has_low.astype(jnp.int32) + 2 * has_high.astype(jnp.int32)
+        barrier, 10 + 2 * has_low.astype(jnp.int32) + 2 * has_high.astype(jnp.int32)
     )
+    plan_round(0)
 
     lane = lax.broadcasted_iota(jnp.int32, (4, 8, 128), 2)
     pending = []
@@ -205,12 +257,11 @@
 
         def relax_both(pos, carry):
             ih, py = pos // 4, pos % 4
-            rows = pl.ds(pl.multiple_of(py * 8, 8), 8)
+            rows_of_py = pl.ds(pl.multiple_of(py * 8, 8), 8)
             if step:
-                field = [state[q, ih, rows, :] for q in range(19)]
+                field = [state[q, ih, rows_of_py, :] for q in range(19)]
             else:
-                flat = raw.at[ih].reshape(768, 128)
-                field = [flat[pl.ds(py * 192 + q, 8, stride=24), :] for q in range(19)]
+                field = [raw[ih, q, rows_of_py, :] for q in range(19)]
             balance = equilibrium(field)
             for_coarse, for_fine = coef[1, py], coef[2, py]
             for q in range(19):
@@ -278,12 +329,20 @@
                 copy.start()
             else:
                 pl.when(send_if)(copy.start)
+        if step == 0:
+            end_round(0)
+            plan_round(1)
         for send_if, recv_if, copy in copies:
             if recv_if is None:
                 copy.wait_recv()
             else:
                 pl.when(recv_if)(copy.wait_recv)
         pending += copies
+        if step == 0:
+            end_round(1)
+            plan_round(2)
+        else:
+            end_round(3)
 
         fine = coef[0] > 0.5
         for q in range(19):
@@ -301,10 +360,14 @@
                 result.append(shifted(main, before, after, q).reshape(4, 4, 8, 128))
             state[q] = jnp.where(fine[None], result[1], result[0]).reshape(4, 32, 128)
 
+        if step == 0:
+            end_round(2)
+            plan_round(3)
+
         def relax_again(pos, carry):
             ih, py = pos // 4, pos % 4
-            rows = pl.ds(pl.multiple_of(py * 8, 8), 8)
-            field = [state[q, ih, rows, :] for q in range(19)]
+            rows_of_py = pl.ds(pl.multiple_of(py * 8, 8), 8)
+            field = [state[q, ih, rows_of_py, :] for q in range(19)]
             balance = equilibrium(field)
             for q in range(19):
                 work[q, ih, py] = field[q] + (1.0 / TAU_FINE) * (balance[q] - field[q])
@@ -316,99 +379,93 @@
             kept = state[q].reshape(4, 4, 8, 128)
             result = jnp.where(inside & fine[None], moved, kept).reshape(4, 32, 128)
             if step == STEPS - 1:
-                x_out[pl.ds(4 * q, 4)] = result
+                rows[pl.ds(4 * q, 4)] = result
             else:
                 state[q] = result
 
-    for send_if, recv_if, copy in pending:
-        if send_if is None:
-            copy.wait_send()
-        else:
-            pl.when(send_if)(copy.wait_send)
-
-
-def row_holder(row):
-    spare = row - 64
-    x, e = spare // 3, spare % 3
-    chip = 16 * x + 4 * ((e + x) % 4) + (e + 3 * x) % 4
-    return jnp.where(row < 64, row, chip), jnp.where(row < 64, 1, 0)
-
-
-def row_of(b, c):
-    x, z, y = b // 16, (b // 4) % 4, b % 4
-    e = (z + 4 - x) % 4
-    spare = (e < 3) & (y == (e + 3 * x) % 4)
-    row = jnp.where(c == 1, b, 64 + 3 * x + e)
-    return row, (c == 1) | spare
-
-
-def migrate_kernel(
-    devices, x_ref, plan_ref, out_ref, plan_all, plan_turned, inv_vec, inv_smem, gathered, ordered,
-    local_sem, plan_send, plan_recv, spread_send, spread_recv, home_send, home_recv,
+    def drain():
+        for send_if, recv_if, copy in pending:
+            if send_if is None:
+                copy.wait_send()
+            else:
+                pl.when(send_if)(copy.wait_send)
+
+    return drain
+
+
+def spare_unit(b):
+    place = (b // 16 + (b // 4) % 4 + b % 4) % 4
+    return jnp.minimum((b // 4) * 3 + place, UNITS - 1), place < 3
+
+
+def chip_at(b, k):
+    dx = k % 4
+    dz = (dx + k // 4) % 4
+    dy = (dz + k // 16) % 4
+    return 16 * ((b // 16 + dx) % 4) + 4 * (((b // 4) % 4 + dz) % 4) + (b % 4 + dy) % 4
+
+
+def quarters(parts, sign):
+    quarter = lax.broadcasted_iota(jnp.int32, parts[0].shape, parts[0].ndim - 1) // 32
+    out = []
+    for h in range(4):
+        total = parts[h]
+        for m in range(4):
+            if m != h:
+                total = jnp.where(quarter == m, wide_roll(parts[m], 32 * (m - h), total.ndim - 1), total)
+        out.append(total)
+    return out
+
+
+def migrate(
+    chips, out_ref, rows, plan_all, plan_turned, inv_vec, inv_smem, gathered, ordered, unit_out, unit_in, unit_back,
+    local_sem, row_send, unit_send, spread_recv, home_send, home_recv, unit_recv,
 ):
     b = lax.axis_index("blocks")
     c = lax.axis_index("cross")
-    me = 2 * b + c
-    my_row, is_mid = row_of(b, c)
-    barrier = pltpu.get_barrier_semaphore()
-
-    def each_other(body):
-        def step(k, carry):
-            other = (me + k) % devices
-            body(other, (other // 2, other % 2))
-            return carry
-
-        lax.fori_loop(1, devices, step, 0)
-
-    each_other(
-        lambda other, device: pl.semaphore_signal(
-            barrier, inc=1, device_id=device, device_id_type=MESH
-        )
-    )
-    plan_all[me] = plan_ref[...]
-    pl.semaphore_wait(barrier, devices - 1)
-
-    def send_plan(other, device):
+    source = 64 * c + b
+    my_unit, has_unit = spare_unit(b)
+    is_spare = (c == 0) & has_unit
+    is_main = c == 1
+
+    def remote(src, dst, send, recv, device):
         pltpu.make_async_remote_copy(
-            src_ref=plan_ref,
-            dst_ref=plan_all.at[me],
-            send_sem=plan_send,
-            recv_sem=plan_recv,
-            device_id=device,
-            device_id_type=MESH,
+            src_ref=src, dst_ref=dst, send_sem=send, recv_sem=recv, device_id=device, device_id_type=MESH
         ).start()
 
-    each_other(send_plan)
-
-    def send_row(k, carry):
-        row = (my_row + 1 + k) % ROWS
-        device = row_holder(row)
-
-        @pl.when((device[0] != b) | (device[1] != c))
+    def block(ref, index, size):
+        return ref.at[pl.ds(pl.multiple_of(index * size, size), size)]
+
+    spare_rows = rows[pl.ds(64, 12)].reshape(12, 4, 8, 128)
+    for h, part in enumerate(quarters([spare_rows[:, m] for m in range(4)], 1)):
+        unit_out[:, h] = part
+
+    def spread(k, carry):
+        chip = chip_at(b, k)
+
+        @pl.when((k > 0) | (c == 0))
         def _():
-            pltpu.make_async_remote_copy(
-                src_ref=x_ref.at[row],
-                dst_ref=gathered.at[pl.ds(pl.multiple_of(me * 32, 32), 32)],
-                send_sem=spread_send,
-                recv_sem=spread_recv,
-                device_id=device,
-                device_id_type=MESH,
-            ).start()
+            remote(rows.at[chip], block(gathered, source, 32), row_send, spread_recv, (chip, 1))
+
+        unit, wanted = spare_unit(chip)
+
+        @pl.when(wanted & ((k > 0) | (c == 1)))
+        def _():
+            remote(unit_out.at[unit // 4, unit % 4], block(unit_in, source, 8), unit_send, spread_recv, (chip, 0))
 
         return carry
 
-    lax.fori_loop(0, ROWS, send_row, 0)
-
-    def wait_for(sem, blocks_of_rows):
-        part = gathered.at[pl.ds(0, 32 * blocks_of_rows)]
+    lax.fori_loop(0, chips, spread, 0)
+
+    def wait_rows(sem, count):
+        part = gathered.at[pl.ds(0, 32 * count)]
         pltpu.make_async_copy(part, part, sem).wait()
 
-    others = plan_all.at[pl.ds(0, devices - 1)]
-    pltpu.make_async_copy(others, others, plan_recv).wait()
-
-    @pl.when(is_mid)
-    def _():
-        gathered[pl.ds(pl.multiple_of(me * 32, 32), 32), :] = x_ref[my_row]
+    def wait_units(sem, count):
+        part = unit_in.at[pl.ds(0, 8 * count)]
+        pltpu.make_async_copy(part, part, sem).wait()
+
+    def find_slots():
         plans = plan_all[:, 0, :]
         plan_turned[...] = plans.T
         sub = lax.broadcasted_iota(jnp.int32, (128, 128), 0)
@@ -429,106 +486,164 @@
 
         _, total = lax.fori_loop(0, 32, place, (plans, jnp.zeros((128, 128), jnp.float32)))
         total = total.astype(jnp.int32)
-        inv_vec[...] = jnp.clip(total * 32 + pltpu.roll(total, 96, 1), 0, 32 * devices - 1)
+        inv_vec[...] = jnp.clip(total * 32 + pltpu.roll(total, 96, 1), 0, 64 * chips - 1)
         move = pltpu.make_async_copy(inv_vec, inv_smem, local_sem)
         move.start()
         move.wait()
-        wait_for(spread_recv, devices - 1)
-
-        def place_at(owner):
-            return ordered.at[pl.ds(pl.multiple_of(owner * 32, 32), 32)]
-
-        def target():
-            return out_ref.at[my_row]
-
-        def send_owner(owner):
-            pltpu.make_async_remote_copy(
-                src_ref=place_at(owner),
-                dst_ref=target(),
-                send_sem=home_send,
-                recv_sem=home_recv,
-                device_id=(owner // 2, owner % 2),
-                device_id_type=MESH,
-            ).start()
-
-        def pick(k, carry):
-            owner = (me + k) % devices
-            for u in range(32):
-                index = inv_smem[owner, u]
-                ordered[pl.ds(owner * 32 + u, 1), :] = gathered[pl.ds(index, 1), :]
+
+    def pick(chip, core):
+        owner = 2 * chip + core
+        for u in range(32):
+            index = inv_smem[owner, u]
+            ordered[pl.ds(owner * 32 + u, 1), :] = gathered[pl.ds(index, 1), :]
+
+    my_place = out_ref.at[b // 4, :, pl.ds(pl.multiple_of((b % 4) * 128, 128), 128)]
+
+    @pl.when(is_main)
+    def _():
+        find_slots()
+        gathered[pl.ds(pl.multiple_of(source * 32, 32), 32), :] = rows[b]
+        wait_rows(spread_recv, 2 * chips - 1)
+
+        def send(chip, core):
+            remote(block(ordered, 2 * chip + core, 32), my_place, home_send, home_recv, (chip, core))
+
+        def step(k, carry):
+            chip = chip_at(b, k % chips)
+            pick(chip, 0)
+            pick(chip, 1)
 
             @pl.when(k > 1)
             def _():
-                send_owner((me + k - 1) % devices)
+                before = chip_at(b, k - 1)
+                send(before, 0)
+                send(before, 1)
 
             return carry
 
-        lax.fori_loop(1, devices + 1, pick, 0)
-        out_ref[my_row] = ordered[pl.ds(pl.multiple_of(me * 32, 32), 32), :]
-        wait_for(home_send, devices - 1)
-        wait_for(spread_send, ROWS - 1)
-        wait_for(home_recv, ROWS - 1)
-
-    @pl.when(jnp.logical_not(is_mid))
+        lax.fori_loop(1, chips + 1, step, 0)
+        out_ref[b // 4, :, pl.ds(pl.multiple_of((b % 4) * 128, 128), 128)] = ordered[
+            pl.ds(pl.multiple_of((2 * b + 1) * 32, 32), 32), :
+        ]
+        send(b, 0)
+        wait_rows(home_send, 2 * chips - 1)
+        wait_rows(row_send, chips - 1)
+        wait_units(unit_send, UNITS)
+        wait_rows(home_recv, chips - 1)
+        wait_units(unit_recv, UNITS)
+
+    @pl.when(is_spare)
     def _():
-        wait_for(spread_send, ROWS)
-        wait_for(home_recv, ROWS)
-
-    pltpu.make_async_copy(others, others, plan_send).wait()
-
-
-def lbm_call(f_home, levels):
-    blocks = lax.axis_size("blocks")
-    vmem = pl.BlockSpec(memory_space=pltpu.VMEM)
-    return pl.pallas_call(
-        lambda *refs: lbm_kernel(blocks, *refs),
-        out_shape=jax.ShapeDtypeStruct((ROWS, 32, 128), jnp.float32),
-        in_specs=[pl.BlockSpec(memory_space=pl.ANY), pl.BlockSpec(memory_space=pltpu.SMEM)],
-        out_specs=vmem,
+        find_slots()
+        unit_in[pl.ds(pl.multiple_of(source * 8, 8), 8), :] = unit_out[my_unit // 4, my_unit % 4]
+        wait_units(spread_recv, 2 * chips - 1)
+
+        def widen(s, carry):
+            part = unit_in[pl.ds(pl.multiple_of(s * 8, 8), 8), :]
+            for m in range(4):
+                gathered[pl.ds(pl.multiple_of(s * 32 + 8 * m, 8), 8), :] = wide_roll(part, -32 * m, 1)
+            return carry
+
+        lax.fori_loop(0, 2 * chips, widen, 0, unroll=4)
+        quarter = lax.broadcasted_iota(jnp.int32, (8, 128), 1) // 32
+
+        def pack(chip, core):
+            owner = 2 * chip + core
+            pick(chip, core)
+            total = ordered[pl.ds(pl.multiple_of(owner * 32, 32), 8), :]
+            for m in (1, 2, 3):
+                part = ordered[pl.ds(pl.multiple_of(owner * 32 + 8 * m, 8), 8), :]
+                total = jnp.where(quarter == m, wide_roll(part, 32 * m, 1), total)
+            unit_in[pl.ds(pl.multiple_of(owner * 8, 8), 8), :] = total
+
+        def send(chip, core):
+            remote(block(unit_in, 2 * chip + core, 8), unit_back.at[my_unit // 4, my_unit % 4], home_send, unit_recv, (chip, core))
+
+        def step(k, carry):
+            chip = chip_at(b, k % chips)
+            pack(chip, 0)
+            pack(chip, 1)
+
+            @pl.when(k > 1)
+            def _():
+                before = chip_at(b, k - 1)
+                send(before, 0)
+                send(before, 1)
+
+            return carry
+
+        lax.fori_loop(1, chips + 1, step, 0)
+        unit_back[my_unit // 4, my_unit % 4] = unit_in[pl.ds(pl.multiple_of(2 * b * 8, 8), 8), :]
+        send(b, 1)
+        wait_units(home_send, 2 * chips - 1)
+        wait_rows(row_send, chips)
+        wait_units(unit_send, UNITS - 1)
+        wait_rows(home_recv, chips)
+        wait_units(unit_recv, UNITS - 1)
+
+    @pl.when((c == 0) & jnp.logical_not(has_unit))
+    def _():
+        wait_rows(row_send, chips)
+        wait_units(unit_send, UNITS)
+        wait_rows(home_recv, chips)
+        wait_units(unit_recv, UNITS)
+
+    back = quarters([unit_back[:, h] for h in range(4)], -1)
+    for n in range(12):
+        q, ih = 16 + n // 4, n % 4
+        for m in range(4):
+            out_ref[q, pl.ds(8 * m, 8), pl.ds(128 * ih, 128)] = back[m][n]
+
+
+def kernel(chips, f_hbm, levels, plan, out_ref, *scratch):
+    rows, plan_all = scratch[:2]
+    drain = lbm_steps(chips, f_hbm, levels, plan, rows, plan_all, *scratch[2:16])
+    migrate(chips, out_ref, rows, plan_all, *scratch[16:])
+    drain()
+
+
+def body(f_home, levels, plan):
+    chips = lax.axis_size("blocks")
+    f32, i32 = jnp.float32, jnp.int32
+    dma = pltpu.SemaphoreType.DMA
+    out = pl.pallas_call(
+        lambda *refs: kernel(chips, *refs),
+        out_shape=jax.ShapeDtypeStruct((19, 32, 512), f32),
+        in_specs=[pl.BlockSpec(memory_space=pltpu.HBM)] * 3,
+        out_specs=pl.BlockSpec(memory_space=pltpu.VMEM),
         scratch_shapes=[
-            pltpu.VMEM((4, 32, 24, 128), jnp.float32),
-            pltpu.VMEM((19, 4, 32, 128), jnp.float32),
-            pltpu.VMEM((STEPS, 2, 19, 4, 6, 8, 128), jnp.float32),
-            pltpu.VMEM((19, 4, 4, 8, 128), jnp.float32),
-            pltpu.VMEM((STEPS, 2, 5, 4, 8, 128), jnp.float32),
-            pltpu.VMEM((STEPS, 2, 5, 6, 8, 128), jnp.float32),
-            pltpu.VMEM((3, 4, 8, 128), jnp.float32),
-            pltpu.SemaphoreType.DMA((4,)),
-            pltpu.SemaphoreType.DMA((STEPS, 16)),
-            pltpu.SemaphoreType.DMA((STEPS, 16)),
-        ],
+            pltpu.VMEM((ROWS, 32, 128), f32),
+            pltpu.VMEM((2 * chips, 1, 128), i32),
+            pltpu.SMEM((32,), i32),
+            pltpu.SMEM((32,), i32),
+            pltpu.VMEM((4, 19, 32, 128), f32),
+            pltpu.VMEM((19, 4, 32, 128), f32),
+            pltpu.VMEM((STEPS, 2, 19, 4, 6, 8, 128), f32),
+            pltpu.VMEM((19, 4, 4, 8, 128), f32),
+            pltpu.VMEM((STEPS, 2, 5, 4, 8, 128), f32),
+            pltpu.VMEM((STEPS, 2, 5, 6, 8, 128), f32),
+            pltpu.VMEM((3, 4, 8, 128), f32),
+            dma((6,)),
+            dma((STEPS, 16)),
+            dma((STEPS, 16)),
+            dma((4,)),
+            dma((4,)),
+            pltpu.VMEM((128, 128), i32),
+            pltpu.VMEM((128, 128), i32),
+            pltpu.SMEM((128, 128), i32),
+            pltpu.VMEM((64 * chips, 128), f32),
+            pltpu.VMEM((64 * chips, 128), f32),
+            pltpu.VMEM((12, 4, 8, 128), f32),
+            pltpu.VMEM((16 * chips, 128), f32),
+            pltpu.VMEM((12, 4, 8, 128), f32),
+        ]
+        + [dma] * 7,
         compiler_params=pltpu.CompilerParams(
-            collective_id=0, has_side_effects=True, vmem_limit_bytes=60 * 1024 * 1024
+            collective_id=0, has_side_effects=True, vmem_limit_bytes=VMEM_LIMIT
         ),
-        name="lbm",
-    )(f_home, levels)
-
-
-def body(f_home, levels, plan):
-    blocks = lax.axis_size("blocks")
-    devices = 2 * blocks
-    vmem = pl.BlockSpec(memory_space=pltpu.VMEM)
-    state = lbm_call(f_home, levels)
-    rows = pl.pallas_call(
-        lambda *refs: migrate_kernel(devices, *refs),
-        out_shape=jax.ShapeDtypeStruct((ROWS, 32, 128), jnp.float32),
-        in_specs=[vmem, vmem],
-        out_specs=vmem,
-        scratch_shapes=[
-            pltpu.VMEM((devices, 1, 128), jnp.int32),
-            pltpu.VMEM((128, 128), jnp.int32),
-            pltpu.VMEM((128, 128), jnp.int32),
-            pltpu.SMEM((128, 128), jnp.int32),
-            pltpu.VMEM((devices * 32, 128), jnp.float32),
-            pltpu.VMEM((devices * 32, 128), jnp.float32),
-        ]
-        + [pltpu.SemaphoreType.DMA] * 7,
-        compiler_params=pltpu.CompilerParams(
-            collective_id=1, has_side_effects=True, vmem_limit_bytes=60 * 1024 * 1024
-        ),
-        name="migrate",
-    )(state, jnp.pad(plan, (0, 96)).reshape(1, 128))
-    return rows.reshape(19, 4, 32, 128).transpose(2, 0, 1, 3).reshape(32, 19, 512)
+        name="lattice_and_owners",
+    )(f_home.transpose(1, 0, 2), levels, plan)
+    return out.transpose(1, 0, 2)
 
 
 def solution(mesh):

time: 104 us -> 70.2 us (0.68)
  the two profiles are of different devices: /device:TPU:101 before, /device:TPU:1 now
where the time goes in v2:
time: 70.2 us; the launch traced here: 70.1 us
  Pallas kernels  66.4 us (95%)
  local copies, waits for them, and re-layouts  3.64 us (5%)
    pallas_call x1, Pallas kernels, body(): pl.pallas_call(lambda *refs: kernel(chips, *refs), out_shape=jax.ShapeDty...  66.4 us
    unnamed x7, local copies, waits for them, and re-layouts  3.64 us

profile of v2, /device:TPU:1, one launch (start us, length us, event | category | flops | bytes accessed | tf_op | source)
XLA Modules:
  0.0 70.1 jit_solution(13236900364577969333)
XLA Ops:
  0.0 0.0 copy-start
  0.0 1.3 %copy-done = f32[32,19,512]{2,0,1:T(8,128)S(1)} copy-done((f32[32,19,512]{2,0,1:T(8,128)S(1)}, f32[32,19,512]{2,0,1:T(8,128)}, u32[]{:S(2)}) %copy-start) | copy-done | bytes 1245208
  1.3 0.0 copy-start.1
  1.3 0.7 copy-done.1
  1.9 0.0 copy-start.2
  2.0 0.7 copy-done.2
  2.6 66.4 %lattice_and_owners.1 = f32[19,32,512]{2,1,0:T(8,128)S(1)} custom-call(f32[19,32,512]{2,1,0:T(8,128)S(1)} %bitcast.3, s32[32]{0:T(128)S(1)} %copy-done.1, s32[32]{0:T(128)S(1)} %copy-done.2), custom_call_target="tpu_custom_call" | custom-call | tf_op jit(solution)/shard_map/lattice_and_owners/pallas_call | solution.py:609
  69.0 1.0 %copy.5 = f32[32,19,512]{2,0,1:T(8,128)} copy(f32[32,19,512]{2,0,1:T(8,128)S(1)} %bitcast.2) | data formatting | bytes 2490368
Async XLA Ops:
  0.0 1.3 %copy-start = (f32[32,19,512]{2,0,1:T(8,128)S(1)}, f32[32,19,512]{2,0,1:T(8,128)}, u32[]{:S(2)}) copy-start(f32[32,19,512]{2,0,1:T(8,128)} %param.3) | copy-start | bytes 3735556
  1.3 0.7 copy-start.1
  1.9 0.7 copy-start.2

commit v3 on v2

--- a/solution.py
+++ b/solution.py
@@ -38,7 +38,7 @@
 INFLOW = 0.08
 ROWS = 76
 UNITS = 48
-VMEM_LIMIT = 28 * 1024 * 1024
+VMEM_LIMIT = 56 * 1024 * 1024
 
 
 def inflow_value(speed):
@@ -94,23 +94,22 @@
     return values if shift == 0 else pltpu.roll(values, shift, axis)
 
 
-def shifted(main, before, after, q):
+def shifted(main, other, q):
     ex, ey, ez = VELOCITIES[q]
+    n = main.shape[0]
     lane, j, k = lattice_masks((1, 8, 128))
     if ex > 0:
-        other = jnp.concatenate([before[None], main[:3]], axis=0)
         main = jnp.where(lane[None] < 64, main, other)
     elif ex < 0:
-        other = jnp.concatenate([main[1:], after[None]], axis=0)
         main = jnp.where(lane[None] >= 64, main, other)
     turn = 64 if ex else 0
-    here = main[:, 1:5].reshape(16, 8, 128)
+    here = main[:, 1:5].reshape(4 * n, 8, 128)
     if ey > 0:
-        there = main[:, 0:4].reshape(16, 8, 128)
+        there = main[:, 0:4].reshape(4 * n, 8, 128)
         here = jnp.where(j > 0, wide_roll(here, turn + 8, 2), wide_roll(there, turn - 56, 2))
         turn = 0
     elif ey < 0:
-        there = main[:, 2:6].reshape(16, 8, 128)
+        there = main[:, 2:6].reshape(4 * n, 8, 128)
         here = jnp.where(j < 7, wide_roll(here, turn - 8, 2), wide_roll(there, turn + 56, 2))
         turn = 0
     if ez > 0:
@@ -121,7 +120,7 @@
         here = jnp.where(k < 7, wide_roll(here, turn - 1, 2), over)
     else:
         here = wide_roll(here, turn, 2)
-    return here
+    return here.reshape(n, 4, 8, 128)
 
 
 def shifted_inside(main, q):
@@ -246,17 +245,27 @@
 
     for load in loads:
         load.wait()
-    pl.semaphore_wait(
-        barrier, 10 + 2 * has_low.astype(jnp.int32) + 2 * has_high.astype(jnp.int32)
-    )
-    plan_round(0)
 
     lane = lax.broadcasted_iota(jnp.int32, (4, 8, 128), 2)
     pending = []
+
+    def over_outer(body):
+        def at(pos, carry):
+            body(3 * (pos // 4), pos % 4)
+            return carry
+
+        lax.fori_loop(0, 8, at, 0)
+
+    def over_inner(body):
+        def at(pos, carry):
+            body(1 + pos // 4, pos % 4)
+            return carry
+
+        lax.fori_loop(0, 8, at, 0)
+
     for step in range(STEPS):
 
-        def relax_both(pos, carry):
-            ih, py = pos // 4, pos % 4
+        def relax_both(ih, py):
             rows_of_py = pl.ds(pl.multiple_of(py * 8, 8), 8)
             if step:
                 field = [state[q, ih, rows_of_py, :] for q in range(19)]
@@ -268,9 +277,8 @@
                 away = field[q] - balance[q]
                 both[step, 0, q, ih, py + 1] = balance[q] + for_coarse * away
                 both[step, 1, q, ih, py + 1] = balance[q] + for_fine * away
-            return carry
-
-        lax.fori_loop(0, 16, relax_both, 0)
+
+        over_outer(relax_both)
 
         copies = []
 
@@ -293,6 +301,10 @@
                 second = pltpu.roll(both[step, 1, q, edge, 1:5], 64, 2)
                 keep = lane >= 64 if side == 0 else lane < 64
                 pack_x[step, side, n] = jnp.where(keep, first, second)
+        if step == 0:
+            pl.semaphore_wait(
+                barrier, 10 + 2 * has_low.astype(jnp.int32) + 2 * has_high.astype(jnp.int32)
+            )
         for side in range(2):
             target = high if side == 0 else low
             send_if, recv_if = (has_high, has_low) if side == 0 else (has_low, has_high)
@@ -314,6 +326,23 @@
                         send_if,
                         recv_if,
                     )
+        def start(chosen):
+            for send_if, recv_if, copy in chosen:
+                if send_if is None:
+                    copy.start()
+                else:
+                    pl.when(send_if)(copy.start)
+
+        def arrive(chosen):
+            for send_if, recv_if, copy in chosen:
+                if recv_if is None:
+                    copy.wait_recv()
+                else:
+                    pl.when(recv_if)(copy.wait_recv)
+
+        start(copies)
+        along_x = len(copies)
+        over_inner(relax_both)
         for side in range(2):
             py, slot = (4, 0) if side == 0 else (1, 5)
             for q in Y_SPEEDS[side]:
@@ -324,56 +353,54 @@
                     None,
                     None,
                 )
-        for send_if, recv_if, copy in copies:
-            if send_if is None:
-                copy.start()
-            else:
-                pl.when(send_if)(copy.start)
+        start(copies[along_x:])
         if step == 0:
-            end_round(0)
-            plan_round(1)
-        for send_if, recv_if, copy in copies:
-            if recv_if is None:
-                copy.wait_recv()
-            else:
-                pl.when(recv_if)(copy.wait_recv)
-        pending += copies
-        if step == 0:
+            plan_round(0)
+        else:
             end_round(1)
             plan_round(2)
-        else:
-            end_round(3)
-
         fine = coef[0] > 0.5
-        for q in range(19):
+
+        def stream(q, first, last, halo):
             ex = VELOCITIES[q][0]
             result = []
             for kind in range(2):
-                before = after = None
-                if ex > 0:
-                    before = halo_x[step, 0, X_SPEEDS[0].index(q)]
-                    before = pltpu.roll(before, 64, 2) if kind else before
-                elif ex < 0:
-                    after = halo_x[step, 1, X_SPEEDS[1].index(q)]
-                    after = pltpu.roll(after, 64, 2) if kind else after
-                main = both[step, kind, q]
-                result.append(shifted(main, before, after, q).reshape(4, 4, 8, 128))
-            state[q] = jnp.where(fine[None], result[1], result[0]).reshape(4, 32, 128)
-
-        if step == 0:
-            end_round(2)
-            plan_round(3)
-
-        def relax_again(pos, carry):
-            ih, py = pos // 4, pos % 4
+                other = None
+                if halo:
+                    side = 0 if ex > 0 else 1
+                    other = halo_x[step, side, X_SPEEDS[side].index(q)]
+                    other = (pltpu.roll(other, 64, 2) if kind else other)[None]
+                elif ex:
+                    other = both[step, kind, q, first - ex : last - ex]
+                result.append(shifted(both[step, kind, q, first:last], other, q))
+            moved = jnp.where(fine[None], result[1], result[0])
+            state[q, first:last] = moved.reshape(last - first, 32, 128)
+
+        arrive(copies[along_x:])
+        for q in range(19):
+            ex = VELOCITIES[q][0]
+            stream(q, 1 if ex > 0 else 0, 3 if ex < 0 else 4, False)
+
+        def relax_again(ih, py):
             rows_of_py = pl.ds(pl.multiple_of(py * 8, 8), 8)
             field = [state[q, ih, rows_of_py, :] for q in range(19)]
             balance = equilibrium(field)
             for q in range(19):
                 work[q, ih, py] = field[q] + (1.0 / TAU_FINE) * (balance[q] - field[q])
-            return carry
-
-        lax.fori_loop(0, 16, relax_again, 0)
+
+        over_inner(relax_again)
+        arrive(copies[:along_x])
+        pending += copies
+        if step == 0:
+            end_round(0)
+            plan_round(1)
+        else:
+            end_round(2)
+            plan_round(3)
+        for side in range(2):
+            for q in X_SPEEDS[side]:
+                stream(q, 3 * side, 3 * side + 1, True)
+        over_outer(relax_again)
         for q in range(19):
             moved, inside = shifted_inside(work[q], q)
             kept = state[q].reshape(4, 4, 8, 128)
@@ -382,6 +409,8 @@
                 rows[pl.ds(4 * q, 4)] = result
             else:
                 state[q] = result
+
+    end_round(3)
 
     def drain():
         for send_if, recv_if, copy in pending:
@@ -608,7 +637,7 @@
     dma = pltpu.SemaphoreType.DMA
     out = pl.pallas_call(
         lambda *refs: kernel(chips, *refs),
-        out_shape=jax.ShapeDtypeStruct((19, 32, 512), f32),
+        out_shape=pltpu.VMEM((19, 32, 512), f32),
         in_specs=[pl.BlockSpec(memory_space=pltpu.HBM)] * 3,
         out_specs=pl.BlockSpec(memory_space=pltpu.VMEM),
         scratch_shapes=[

time: 70.2 us -> 60.6 us (0.86)
  Pallas kernels: 66.4 us -> 59.4 us
  local copies, waits for them, and re-layouts: 3.64 us -> 1.04 us
    pallas_call x1, Pallas kernels: 66.4 us -> 59.4 us  [body(): pl.pallas_call(lambda *refs: kernel(chips, *refs), out_shape=pltpu.VMEM((...]
    unnamed x7 -> x1, local copies, waits for them, and re-layouts: 3.64 us -> 1.04 us
where the time goes in v3:
time: 60.6 us; the launch traced here: 60.4 us
  Pallas kernels  59.4 us (98%)
  local copies, waits for them, and re-layouts  1.04 us (2%)
    pallas_call x1, Pallas kernels, body(): pl.pallas_call(lambda *refs: kernel(chips, *refs), out_shape=pltpu.VMEM((...  59.4 us

profile of v3, /device:TPU:1, one launch (start us, length us, event | category | flops | bytes accessed | tf_op | source)
XLA Modules:
  0.0 60.4 jit_solution(16842126840190880028)
XLA Ops:
  0.0 59.4 %lattice_and_owners.1 = f32[19,32,512]{2,1,0:T(8,128)S(1)} custom-call(f32[19,32,512]{2,1,0:T(8,128)} %bitcast.3, s32[32]{0:T(128)} %refs_1_.1, s32[32]{0:T(128)} %refs_2_.1), custom_call_target="tpu_custom_call" | custom-call | tf_op jit(solution)/shard_map/lattice_and_owners/pallas_call | solution.py:638
  59.4 1.0 %copy.5 = f32[32,19,512]{2,0,1:T(8,128)} copy(f32[32,19,512]{2,0,1:T(8,128)S(1)} %bitcast.2) | data formatting | bytes 2490368

commit v4 on v3

--- a/solution.py
+++ b/solution.py
@@ -36,9 +36,35 @@
 TAU_FINE = 2.0 * TAU_COARSE - 0.5
 RESCALE = TAU_FINE / (2.0 * TAU_COARSE)
 INFLOW = 0.08
-ROWS = 76
-UNITS = 48
+
+
+def row_units():
+    early, late = [], []
+    for q in range(19):
+        for ih in range(4):
+            ready = ((1, 2), (2,), (1,))[VELOCITIES[q][0]]
+            (early if ih in ready else late).append((q, ih))
+    chips = []
+    for b in range(64):
+        x, z, y = b // 16, b // 4 % 4, b % 4
+        if (x + z) % 2 or y != (x + z) % 4:
+            chips.append(b)
+    units = {}
+    for n, row in enumerate(early):
+        units[row] = ("early", chips[2 * n : 2 * n + 2])
+    for n, row in enumerate(late):
+        units[row] = ("late", n)
+    return units
+
+
+UNITS = row_units()
+EARLY = 56
 VMEM_LIMIT = 56 * 1024 * 1024
+
+
+def has_early(b):
+    x, z, y = b // 16, (b // 4) % 4, b % 4
+    return ((x + z) % 2 == 1) | (y != (x + z) % 4)
 
 
 def inflow_value(speed):
@@ -123,32 +149,53 @@
     return here.reshape(n, 4, 8, 128)
 
 
-def shifted_inside(main, q):
+def lane_blocks(parts):
+    n = len(parts)
+    section = lax.broadcasted_iota(jnp.int32, parts[0].shape, parts[0].ndim - 1) // (128 // n)
+    out = []
+    for h in range(n):
+        total = parts[h]
+        for m in range(n):
+            if m != h:
+                total = jnp.where(section == m, wide_roll(parts[m], 128 // n * (m - h), total.ndim - 1), total)
+        out.append(total)
+    return out
+
+
+def chosen(parts):
+    section = lax.broadcasted_iota(jnp.int32, (8, 128), 1) // 32
+    total = None
+    for h, (part, at) in enumerate(parts):
+        part = wide_roll(part, 32 * (h - at), 1)
+        total = part if total is None else jnp.where(section == h, part, total)
+    return total
+
+
+def shifted_inside(work, q, ih):
     ex, ey, ez = VELOCITIES[q]
-    shape = (4, 1, 8, 128)
-    lane, j, k = lattice_masks(shape)
-    high = lax.broadcasted_iota(jnp.int32, shape, 0)
-    inside = lane >= 0
-    if ex > 0:
-        other = jnp.concatenate([main[:1], main[:3]], axis=0)
-        main = jnp.where(lane < 64, main, other)
-        inside = inside & (high * 128 + lane >= 64)
-    elif ex < 0:
-        other = jnp.concatenate([main[1:], main[3:]], axis=0)
-        main = jnp.where(lane >= 64, main, other)
-        inside = inside & (high * 128 + lane < 448)
+    lane, j, k = lattice_masks((1, 8, 128))
+    main = work[q, ih]
+    inside = None
+
+    def both_of(first, second):
+        return second if first is None else first & second
+
+    if ex:
+        low = lane < 64
+        if 0 <= ih - ex < 4:
+            main = jnp.where(low if ex > 0 else ~low, main, work[q, ih - ex])
+        else:
+            inside = ~low if ex > 0 else low
     if ey:
-        inside = inside & ((j > 0) if ey > 0 else (j < 7))
+        inside = both_of(inside, (j > 0) if ey > 0 else (j < 7))
     if ez:
-        inside = inside & ((k > 0) if ez > 0 else (k < 7))
-    turn = (64 if ex else 0) + 8 * ey + ez
-    moved = wide_roll(main.reshape(16, 8, 128), turn, 2)
-    return moved.reshape(4, 4, 8, 128), inside
+        inside = both_of(inside, (k > 0) if ez > 0 else (k < 7))
+    return wide_roll(main, (64 if ex else 0) + 8 * ey + ez, 2), inside
 
 
 def lbm_steps(
-    blocks, f_hbm, levels_hbm, plan_hbm, rows, plan_all, levels, plan, raw, state, both, work, pack_x, halo_x, coef,
-    load_sem, send_sem, recv_sem, round_send, round_recv,
+    blocks, f_hbm, levels_hbm, plan_hbm, sends, late_rows, plan_all, levels, plan, raw, state, both, work, pack_x, halo_x, coef,
+    load_sem, send_sem, recv_sem, round_send, round_recv, ready, send_early,
 ):
     b = lax.axis_index("blocks")
     c = lax.axis_index("cross")
@@ -175,6 +222,15 @@
 
     greet((b, 1 - c))
 
+    def line(axis):
+        stride = (16, 4, 1)[axis]
+        at = (b // stride) % 4
+        return [b + stride * ((at + k) % 4 - at) for k in (1, 2, 3)]
+
+    for axis in range(3):
+        for chip in line(axis):
+            greet((chip, c))
+
     @pl.when(has_low)
     def _():
         greet((low, c))
@@ -210,15 +266,6 @@
     for p in range(32):
         plan_row = jnp.where(plan_lane == p, plan[p], plan_row)
     plan_all[64 * c + b] = plan_row
-
-    def line(axis):
-        stride = (16, 4, 1)[axis]
-        at = (b // stride) % 4
-        return [b + stride * ((at + k) % 4 - at) for k in (1, 2, 3)]
-
-    for axis in range(3):
-        for chip in line(axis):
-            greet((chip, c))
 
     def plan_round(number):
         size = (1, 4, 16, 64)[number]
@@ -305,6 +352,8 @@
             pl.semaphore_wait(
                 barrier, 10 + 2 * has_low.astype(jnp.int32) + 2 * has_high.astype(jnp.int32)
             )
+            for chip in line(2):
+                pl.semaphore_signal(ready.at[0], inc=1, device_id=(chip, c), device_id_type=MESH)
         for side in range(2):
             target = high if side == 0 else low
             send_if, recv_if = (has_high, has_low) if side == 0 else (has_low, has_high)
@@ -359,7 +408,7 @@
         else:
             end_round(1)
             plan_round(2)
-        fine = coef[0] > 0.5
+        fine = coef[0]
 
         def stream(q, first, last, halo):
             ex = VELOCITIES[q][0]
@@ -373,7 +422,7 @@
                 elif ex:
                     other = both[step, kind, q, first - ex : last - ex]
                 result.append(shifted(both[step, kind, q, first:last], other, q))
-            moved = jnp.where(fine[None], result[1], result[0])
+            moved = jnp.where(fine[None] > 0.5, result[1], result[0])
             state[q, first:last] = moved.reshape(last - first, 32, 128)
 
         arrive(copies[along_x:])
@@ -388,12 +437,39 @@
             for q in range(19):
                 work[q, ih, py] = field[q] + (1.0 / TAU_FINE) * (balance[q] - field[q])
 
+        def finish(q, ih):
+            moved, inside = shifted_inside(work, q, ih)
+            inside = fine > 0.5 if inside is None else inside & (fine > 0.5)
+            result = jnp.where(inside, moved, state[q, ih].reshape(4, 8, 128)).reshape(32, 128)
+            if step == STEPS - 1:
+                kind, place = UNITS[q, ih]
+                if kind == "late":
+                    late_rows[place] = result
+                else:
+                    for chip, block in zip(place, lane_blocks([result[:16], result[16:]])):
+                        sends[kind][chip] = block
+            else:
+                state[q, ih] = result
+
+        if step == 0:
+            pl.semaphore_wait(ready.at[0], 3)
+            for chip in line(1):
+                pl.semaphore_signal(ready.at[1], inc=1, device_id=(chip, c), device_id_type=MESH)
         over_inner(relax_again)
+        last = step == STEPS - 1
+        early = [row for row, unit in UNITS.items() if unit[0] == "early"]
+        if last:
+            for q, ih in early:
+                finish(q, ih)
+            pl.semaphore_wait(ready.at[2], 1)
+            send_early()
         arrive(copies[:along_x])
         pending += copies
         if step == 0:
             end_round(0)
             plan_round(1)
+            pl.semaphore_wait(ready.at[1], 3)
+            pl.semaphore_signal(ready.at[2], inc=1, device_id=(b, 1 - c), device_id_type=MESH)
         else:
             end_round(2)
             plan_round(3)
@@ -402,15 +478,9 @@
                 stream(q, 3 * side, 3 * side + 1, True)
         over_outer(relax_again)
         for q in range(19):
-            moved, inside = shifted_inside(work[q], q)
-            kept = state[q].reshape(4, 4, 8, 128)
-            result = jnp.where(inside & fine[None], moved, kept).reshape(4, 32, 128)
-            if step == STEPS - 1:
-                rows[pl.ds(4 * q, 4)] = result
-            else:
-                state[q] = result
-
-    end_round(3)
+            for ih in range(4):
+                if not (last and (q, ih) in early):
+                    finish(q, ih)
 
     def drain():
         for send_if, recv_if, copy in pending:
@@ -419,123 +489,134 @@
             else:
                 pl.when(send_if)(copy.wait_send)
 
-    return drain
-
-
-def spare_unit(b):
-    place = (b // 16 + (b // 4) % 4 + b % 4) % 4
-    return jnp.minimum((b // 4) * 3 + place, UNITS - 1), place < 3
+    return drain, lambda: end_round(3)
 
 
 def chip_at(b, k):
-    dx = k % 4
-    dz = (dx + k // 4) % 4
-    dy = (dz + k // 16) % 4
-    return 16 * ((b // 16 + dx) % 4) + 4 * (((b // 4) % 4 + dz) % 4) + (b % 4 + dy) % 4
-
-
-def quarters(parts, sign):
-    quarter = lax.broadcasted_iota(jnp.int32, parts[0].shape, parts[0].ndim - 1) // 32
-    out = []
-    for h in range(4):
-        total = parts[h]
-        for m in range(4):
-            if m != h:
-                total = jnp.where(quarter == m, wide_roll(parts[m], 32 * (m - h), total.ndim - 1), total)
-        out.append(total)
-    return out
-
-
-def migrate(
-    chips, out_ref, rows, plan_all, plan_turned, inv_vec, inv_smem, gathered, ordered, unit_out, unit_in, unit_back,
-    local_sem, row_send, unit_send, spread_recv, home_send, home_recv, unit_recv,
-):
+    def mod(value):
+        return lax.rem(value, jnp.int32(4))
+
+    def div(value, by):
+        return lax.div(value, jnp.int32(by))
+
+    dx = mod(k)
+    dz = dx + div(k, 4)
+    dy = dz + div(k, 16)
+    return 16 * mod(div(b, 16) + dx) + 4 * mod(div(b, 4) + dz) + mod(b + dy)
+
+
+def migrate(chips, sends, late_rows, plan_all, homes, plan_turned, inv_vec, inv_smem, wide, ordered, outs, local_sem, sems):
     b = lax.axis_index("blocks")
     c = lax.axis_index("cross")
     source = 64 * c + b
-    my_unit, has_unit = spare_unit(b)
-    is_spare = (c == 0) & has_unit
-    is_main = c == 1
+    cores = {"early": 1, "late": 0}
+    sizes = {"early": 16, "late": 24}
 
     def remote(src, dst, send, recv, device):
         pltpu.make_async_remote_copy(
             src_ref=src, dst_ref=dst, send_sem=send, recv_sem=recv, device_id=device, device_id_type=MESH
         ).start()
 
-    def block(ref, index, size):
-        return ref.at[pl.ds(pl.multiple_of(index * size, size), size)]
-
-    spare_rows = rows[pl.ds(64, 12)].reshape(12, 4, 8, 128)
-    for h, part in enumerate(quarters([spare_rows[:, m] for m in range(4)], 1)):
-        unit_out[:, h] = part
-
-    def spread(k, carry):
+    def wait_for(kind, sem, count):
+        part = wide.at[pl.ds(0, sizes[kind] * count)]
+        pltpu.make_async_copy(part, part, sems.at[sem]).wait()
+
+    number = {"early": 0, "late": 4}
+
+    def spread(kind, chip, k):
+        @pl.when((k > 0) | (c != cores[kind]))
+        def _():
+            n = number[kind]
+            land = wide.at[pl.ds(pl.multiple_of(source * 32, 32), sizes[kind])]
+            remote(sends[kind].at[chip], land, sems.at[n], sems.at[n + 1], (chip, cores[kind]))
+
+    def send_early():
+        def step(k, carry):
+            chip = chip_at(b, k)
+            pl.when(has_early(chip))(lambda: spread("early", chip, k))
+            return carry
+
+        lax.fori_loop(0, chips, step, 0)
+
+    end_plan = yield send_early
+
+    for chip in range(64):
+        columns = [divmod(3 * chip + i, 4) for i in range(3)]
+        for m in range(3):
+            parts = [(late_rows[n, 8 * m : 8 * m + 8], h) for n, h in columns]
+            n, h = columns[m]
+            sends["late"][chip, 8 * m : 8 * m + 8] = chosen(parts + [(late_rows[n, 24:32], h)])
+
+    def send_late(k, carry):
         chip = chip_at(b, k)
-
-        @pl.when((k > 0) | (c == 0))
-        def _():
-            remote(rows.at[chip], block(gathered, source, 32), row_send, spread_recv, (chip, 1))
-
-        unit, wanted = spare_unit(chip)
-
-        @pl.when(wanted & ((k > 0) | (c == 1)))
-        def _():
-            remote(unit_out.at[unit // 4, unit % 4], block(unit_in, source, 8), unit_send, spread_recv, (chip, 0))
-
+        spread("late", chip, k)
         return carry
 
-    lax.fori_loop(0, chips, spread, 0)
-
-    def wait_rows(sem, count):
-        part = gathered.at[pl.ds(0, 32 * count)]
-        pltpu.make_async_copy(part, part, sem).wait()
-
-    def wait_units(sem, count):
-        part = unit_in.at[pl.ds(0, 8 * count)]
-        pltpu.make_async_copy(part, part, sem).wait()
-
-    def find_slots():
-        plans = plan_all[:, 0, :]
-        plan_turned[...] = plans.T
-        sub = lax.broadcasted_iota(jnp.int32, (128, 128), 0)
-        lane = lax.broadcasted_iota(jnp.int32, (128, 128), 1)
-
-        def place(p, carry):
-            plans, total = carry
-            owner = plan_turned[pl.ds(p, 1), :] // 32
-            hot = jnp.where(owner == sub, 1.0, 0.0)
-            slot = plans[:, 0:1] % 32
-            value = jnp.where(slot == lane, sub, jnp.where(slot + 32 == lane, p, 0))
-            total = total + jnp.dot(
-                hot.astype(jnp.bfloat16),
-                value.astype(jnp.float32).astype(jnp.bfloat16),
-                preferred_element_type=jnp.float32,
-            )
-            return pltpu.roll(plans, 127, 1), total
-
-        _, total = lax.fori_loop(0, 32, place, (plans, jnp.zeros((128, 128), jnp.float32)))
-        total = total.astype(jnp.int32)
-        inv_vec[...] = jnp.clip(total * 32 + pltpu.roll(total, 96, 1), 0, 64 * chips - 1)
-        move = pltpu.make_async_copy(inv_vec, inv_smem, local_sem)
-        move.start()
-        move.wait()
-
-    def pick(chip, core):
-        owner = 2 * chip + core
-        for u in range(32):
-            index = inv_smem[owner, u]
-            ordered[pl.ds(owner * 32 + u, 1), :] = gathered[pl.ds(index, 1), :]
-
-    my_place = out_ref.at[b // 4, :, pl.ds(pl.multiple_of((b % 4) * 128, 128), 128)]
-
-    @pl.when(is_main)
-    def _():
-        find_slots()
-        gathered[pl.ds(pl.multiple_of(source * 32, 32), 32), :] = rows[b]
-        wait_rows(spread_recv, 2 * chips - 1)
-
-        def send(chip, core):
-            remote(block(ordered, 2 * chip + core, 32), my_place, home_send, home_recv, (chip, core))
+    lax.fori_loop(0, chips, send_late, 0)
+    end_plan()
+
+    plans = plan_all[:, 0, :]
+    plan_turned[...] = plans.T
+    sub = lax.broadcasted_iota(jnp.int32, (128, 128), 0)
+    lane = lax.broadcasted_iota(jnp.int32, (128, 128), 1)
+
+    def place(p, carry):
+        plans, total = carry
+        owner = plan_turned[pl.ds(p, 1), :] // 32
+        hot = jnp.where(owner == sub, 1.0, 0.0)
+        slot = plans[:, 0:1] % 32
+        value = jnp.where(slot == lane, sub, jnp.where(slot + 32 == lane, p, 0))
+        total = total + jnp.dot(
+            hot.astype(jnp.bfloat16),
+            value.astype(jnp.float32).astype(jnp.bfloat16),
+            preferred_element_type=jnp.float32,
+        )
+        return pltpu.roll(plans, 127, 1), total
+
+    _, total = lax.fori_loop(0, 32, place, (plans, jnp.zeros((128, 128), jnp.float32)), unroll=4)
+    total = total.astype(jnp.int32)
+    inv_vec[...] = jnp.clip(total * 32 + pltpu.roll(total, 96, 1), 0, 64 * chips - 1)
+    move = pltpu.make_async_copy(inv_vec, inv_smem, local_sem)
+    move.start()
+    move.wait()
+
+    def serve(kind):
+        out, size, n = outs[kind], sizes[kind], number[kind]
+        core = cores[kind]
+        wide[pl.ds(pl.multiple_of(source * 32, 32), size), :] = sends[kind][b]
+        wait_for(kind, n + 1, 2 * chips - 1)
+        section = lax.broadcasted_iota(jnp.int32, (8, 128), 1) // 32
+
+        def widen(s, carry):
+            at = lambda m: pl.ds(pl.multiple_of(s * 32 + 8 * m, 8), 8)
+            if kind == "early":
+                for m in range(2):
+                    wide[at(2 + m), :] = wide_roll(wide[at(m), :], 64, 1)
+            else:
+                wide[at(3), :] = chosen([(wide[at(m), :], 3) for m in range(3)])
+            return carry
+
+        lax.fori_loop(0, 2 * chips, widen, 0, unroll=8)
+
+        def pick(chip, target_core):
+            owner = 2 * chip + target_core
+            for u in range(32):
+                index = inv_smem[owner, u]
+                ordered[pl.ds(owner * 32 + u, 1), :] = wide[pl.ds(index, 1), :]
+            blocks = [ordered[pl.ds(pl.multiple_of(owner * 32 + 8 * m, 8), 8), :] for m in range(4)]
+            if kind == "early":
+                for m in range(2):
+                    out[owner, 8 * m : 8 * m + 8] = jnp.where(
+                        section < 2, blocks[m], wide_roll(blocks[2 + m], 64, 1)
+                    )
+            else:
+                for m in range(3):
+                    out[owner, 8 * m : 8 * m + 8] = jnp.where(
+                        section < 3, blocks[m], wide_roll(blocks[3], 32 * (3 - m), 1)
+                    )
+
+        def send(chip, target_core):
+            remote(out.at[2 * chip + target_core], homes[kind].at[b], sems.at[n + 2], sems.at[n + 3], (chip, target_core))
 
         def step(k, carry):
             chip = chip_at(b, k % chips)
@@ -551,84 +632,63 @@
             return carry
 
         lax.fori_loop(1, chips + 1, step, 0)
-        out_ref[b // 4, :, pl.ds(pl.multiple_of((b % 4) * 128, 128), 128)] = ordered[
-            pl.ds(pl.multiple_of((2 * b + 1) * 32, 32), 32), :
-        ]
-        send(b, 0)
-        wait_rows(home_send, 2 * chips - 1)
-        wait_rows(row_send, chips - 1)
-        wait_units(unit_send, UNITS)
-        wait_rows(home_recv, chips - 1)
-        wait_units(unit_recv, UNITS)
-
-    @pl.when(is_spare)
-    def _():
-        find_slots()
-        unit_in[pl.ds(pl.multiple_of(source * 8, 8), 8), :] = unit_out[my_unit // 4, my_unit % 4]
-        wait_units(spread_recv, 2 * chips - 1)
-
-        def widen(s, carry):
-            part = unit_in[pl.ds(pl.multiple_of(s * 8, 8), 8), :]
-            for m in range(4):
-                gathered[pl.ds(pl.multiple_of(s * 32 + 8 * m, 8), 8), :] = wide_roll(part, -32 * m, 1)
-            return carry
-
-        lax.fori_loop(0, 2 * chips, widen, 0, unroll=4)
-        quarter = lax.broadcasted_iota(jnp.int32, (8, 128), 1) // 32
-
-        def pack(chip, core):
-            owner = 2 * chip + core
-            pick(chip, core)
-            total = ordered[pl.ds(pl.multiple_of(owner * 32, 32), 8), :]
-            for m in (1, 2, 3):
-                part = ordered[pl.ds(pl.multiple_of(owner * 32 + 8 * m, 8), 8), :]
-                total = jnp.where(quarter == m, wide_roll(part, 32 * m, 1), total)
-            unit_in[pl.ds(pl.multiple_of(owner * 8, 8), 8), :] = total
-
-        def send(chip, core):
-            remote(block(unit_in, 2 * chip + core, 8), unit_back.at[my_unit // 4, my_unit % 4], home_send, unit_recv, (chip, core))
-
-        def step(k, carry):
-            chip = chip_at(b, k % chips)
-            pack(chip, 0)
-            pack(chip, 1)
-
-            @pl.when(k > 1)
+        homes[kind][b] = out[2 * b + core]
+        send(b, 1 - core)
+
+    my_early = (c == 1) & has_early(b)
+    pl.when(c == 1)(lambda: wait_for("late", number["late"], chips))
+    pl.when(my_early)(lambda: serve("early"))
+    pl.when(c == 0)(lambda: serve("late"))
+
+    def finish(kind, mine, count):
+        n = number[kind]
+        for holds, held in ((True, mine), (False, jnp.logical_not(mine))):
+
+            @pl.when(held)
             def _():
-                before = chip_at(b, k - 1)
-                send(before, 0)
-                send(before, 1)
-
-            return carry
-
-        lax.fori_loop(1, chips + 1, step, 0)
-        unit_back[my_unit // 4, my_unit % 4] = unit_in[pl.ds(pl.multiple_of(2 * b * 8, 8), 8), :]
-        send(b, 1)
-        wait_units(home_send, 2 * chips - 1)
-        wait_rows(row_send, chips)
-        wait_units(unit_send, UNITS - 1)
-        wait_rows(home_recv, chips)
-        wait_units(unit_recv, UNITS - 1)
-
-    @pl.when((c == 0) & jnp.logical_not(has_unit))
-    def _():
-        wait_rows(row_send, chips)
-        wait_units(unit_send, UNITS)
-        wait_rows(home_recv, chips)
-        wait_units(unit_recv, UNITS)
-
-    back = quarters([unit_back[:, h] for h in range(4)], -1)
-    for n in range(12):
-        q, ih = 16 + n // 4, n % 4
-        for m in range(4):
-            out_ref[q, pl.ds(8 * m, 8), pl.ds(128 * ih, 128)] = back[m][n]
+                wait_for(kind, n + 3, count - holds)
+                if kind == "early" or holds:
+                    wait_for(kind, n, count - holds)
+                if holds:
+                    wait_for(kind, n + 2, 2 * chips - 1)
+
+    return finish, my_early, c
 
 
 def kernel(chips, f_hbm, levels, plan, out_ref, *scratch):
-    rows, plan_all = scratch[:2]
-    drain = lbm_steps(chips, f_hbm, levels, plan, rows, plan_all, *scratch[2:16])
-    migrate(chips, out_ref, rows, plan_all, *scratch[16:])
+    kinds = ("early", "late")
+    take = iter(scratch)
+    plan_all = next(take)
+    lbm = [next(take) for _ in range(15)]
+    sends, homes, outs = ({kind: next(take) for kind in kinds} for _ in range(3))
+    wide, ordered, late_rows = next(take), next(take), next(take)
+    plan_turned, inv_vec, inv_smem, local_sem, sems = take
+    moving = migrate(chips, sends, late_rows, plan_all, homes, plan_turned, inv_vec, inv_smem, wide, ordered, outs, local_sem, sems)
+    send_early = next(moving)
+    drain, end_plan = lbm_steps(chips, f_hbm, levels, plan, sends, late_rows, plan_all, *lbm, send_early)
+    try:
+        moving.send(end_plan)
+    except StopIteration as stop:
+        finish, my_early, c = stop.value
     drain()
+    for kind, mine, count in (("early", my_early, EARLY), ("late", c == 0, chips)):
+        finish(kind, mine, count)
+        for (q, ih), (where, place) in UNITS.items():
+            if where != kind:
+                continue
+            lanes = pl.ds(128 * ih, 128)
+            home = homes[kind]
+            if kind == "early":
+                first, second = lane_blocks([home[chip] for chip in place])
+                out_ref[q, 0:16, lanes] = first
+                out_ref[q, 16:32, lanes] = second
+            else:
+                columns = [divmod(4 * place + h, 3) for h in range(4)]
+                for m in range(3):
+                    out_ref[q, 8 * m : 8 * m + 8, lanes] = chosen(
+                        [(home[chip, 8 * m : 8 * m + 8], i) for chip, i in columns]
+                    )
+                out_ref[q, 24:32, lanes] = chosen([(home[chip, 8 * i : 8 * i + 8], 3) for chip, i in columns])
 
 
 def body(f_home, levels, plan):
@@ -641,7 +701,6 @@
         in_specs=[pl.BlockSpec(memory_space=pltpu.HBM)] * 3,
         out_specs=pl.BlockSpec(memory_space=pltpu.VMEM),
         scratch_shapes=[
-            pltpu.VMEM((ROWS, 32, 128), f32),
             pltpu.VMEM((2 * chips, 1, 128), i32),
             pltpu.SMEM((32,), i32),
             pltpu.SMEM((32,), i32),
@@ -657,16 +716,20 @@
             dma((STEPS, 16)),
             dma((4,)),
             dma((4,)),
+            pltpu.SemaphoreType.REGULAR((3,)),
+        ]
+        + [pltpu.VMEM((64, size, 128), f32) for size in (16, 24)]
+        + [pltpu.VMEM((64, size, 128), f32) for size in (16, 24)]
+        + [pltpu.VMEM((2 * chips, size, 128), f32) for size in (16, 24)]
+        + [pltpu.VMEM((64 * chips, 128), f32)] * 2
+        + [pltpu.VMEM((48, 32, 128), f32)]
+        + [
             pltpu.VMEM((128, 128), i32),
             pltpu.VMEM((128, 128), i32),
             pltpu.SMEM((128, 128), i32),
-            pltpu.VMEM((64 * chips, 128), f32),
-            pltpu.VMEM((64 * chips, 128), f32),
-            pltpu.VMEM((12, 4, 8, 128), f32),
-            pltpu.VMEM((16 * chips, 128), f32),
-            pltpu.VMEM((12, 4, 8, 128), f32),
-        ]
-        + [dma] * 7,
+            dma,
+            dma((8,)),
+        ],
         compiler_params=pltpu.CompilerParams(
             collective_id=0, has_side_effects=True, vmem_limit_bytes=VMEM_LIMIT
         ),

time: 60.6 us -> 59.1 us (0.975)
  Pallas kernels: 59.4 us -> 58 us
    pallas_call x1, Pallas kernels: 59.4 us -> 58 us  [body(): pl.pallas_call(lambda *refs: kernel(chips, *refs), out_shape=pltpu.VMEM((...]
where the time goes in v4:
time: 59.1 us; the launch traced here: 59 us
  Pallas kernels  58 us (98%)
  local copies, waits for them, and re-layouts  1.04 us (2%)
    pallas_call x1, Pallas kernels, body(): pl.pallas_call(lambda *refs: kernel(chips, *refs), out_shape=pltpu.VMEM((...  58 us

profile of v4, /device:TPU:1, one launch (start us, length us, event | category | flops | bytes accessed | tf_op | source)
XLA Modules:
  0.0 59.0 jit_solution(9596475331829293838)
XLA Ops:
  0.0 58.0 %lattice_and_owners.1 = f32[19,32,512]{2,1,0:T(8,128)S(1)} custom-call(f32[19,32,512]{2,1,0:T(8,128)} %bitcast.3, s32[32]{0:T(128)} %refs_1_.1, s32[32]{0:T(128)} %refs_2_.1), custom_call_target="tpu_custom_call" | custom-call | tf_op jit(solution)/shard_map/lattice_and_owners/pallas_call | solution.py:698
  58.0 1.0 %copy.5 = f32[32,19,512]{2,0,1:T(8,128)} copy(f32[32,19,512]{2,0,1:T(8,128)S(1)} %bitcast.2) | data formatting | bytes 2490368

commit v5 on v4

--- a/solution.py
+++ b/solution.py
@@ -63,8 +63,8 @@
 
 
 def has_early(b):
-    x, z, y = b // 16, (b // 4) % 4, b % 4
-    return ((x + z) % 2 == 1) | (y != (x + z) % 4)
+    diagonal = mod(div(b, 16) + div(b, 4))
+    return (lax.rem(diagonal, jnp.int32(2)) == 1) | (mod(b) != diagonal)
 
 
 def inflow_value(speed):
@@ -492,17 +492,26 @@
     return drain, lambda: end_round(3)
 
 
+def mod(value):
+    return lax.rem(value, jnp.int32(4))
+
+
+def div(value, by):
+    return lax.div(value, jnp.int32(by))
+
+
+def chip_beside(b, dx, dz, dy):
+    return 16 * mod(div(b, 16) + dx) + 4 * mod(div(b, 4) + dz) + mod(b + dy)
+
+
 def chip_at(b, k):
-    def mod(value):
-        return lax.rem(value, jnp.int32(4))
-
-    def div(value, by):
-        return lax.div(value, jnp.int32(by))
-
-    dx = mod(k)
-    dz = dx + div(k, 4)
-    dy = dz + div(k, 16)
-    return 16 * mod(div(b, 16) + dx) + 4 * mod(div(b, 4) + dz) + mod(b + dy)
+    dz = k + div(k, 4)
+    return chip_beside(b, k, dz, dz + div(k, 16))
+
+
+OFFSETS = [
+    (k % 4, (k + k // 4) % 4, (k + k // 4 + k // 16) % 4) for k in (*range(63, 0, -1), 0)
+]
 
 
 def migrate(chips, sends, late_rows, plan_all, homes, plan_turned, inv_vec, inv_smem, wide, ordered, outs, local_sem, sems):
@@ -523,20 +532,25 @@
 
     number = {"early": 0, "late": 4}
 
-    def spread(kind, chip, k):
-        @pl.when((k > 0) | (c != cores[kind]))
-        def _():
+    def spread(kind, offset):
+        chip = chip_beside(b, *offset)
+
+        def send():
             n = number[kind]
             land = wide.at[pl.ds(pl.multiple_of(source * 32, 32), sizes[kind])]
             remote(sends[kind].at[chip], land, sems.at[n], sems.at[n + 1], (chip, cores[kind]))
 
+        if kind == "early":
+            wanted = has_early(chip)
+            pl.when(wanted if any(offset) else wanted & (c != cores[kind]))(send)
+        elif any(offset):
+            send()
+        else:
+            pl.when(c != cores[kind])(send)
+
     def send_early():
-        def step(k, carry):
-            chip = chip_at(b, k)
-            pl.when(has_early(chip))(lambda: spread("early", chip, k))
-            return carry
-
-        lax.fori_loop(0, chips, step, 0)
+        for offset in OFFSETS:
+            spread("early", offset)
 
     end_plan = yield send_early
 
@@ -547,12 +561,8 @@
             n, h = columns[m]
             sends["late"][chip, 8 * m : 8 * m + 8] = chosen(parts + [(late_rows[n, 24:32], h)])
 
-    def send_late(k, carry):
-        chip = chip_at(b, k)
-        spread("late", chip, k)
-        return carry
-
-    lax.fori_loop(0, chips, send_late, 0)
+    for offset in OFFSETS:
+        spread("late", offset)
     end_plan()
 
     plans = plan_all[:, 0, :]
@@ -618,20 +628,19 @@
         def send(chip, target_core):
             remote(out.at[2 * chip + target_core], homes[kind].at[b], sems.at[n + 2], sems.at[n + 3], (chip, target_core))
 
-        def step(k, carry):
-            chip = chip_at(b, k % chips)
+        def step(k, before):
+            chip = chip_at(b, chips - k)
             pick(chip, 0)
             pick(chip, 1)
 
             @pl.when(k > 1)
             def _():
-                before = chip_at(b, k - 1)
                 send(before, 0)
                 send(before, 1)
 
-            return carry
-
-        lax.fori_loop(1, chips + 1, step, 0)
+            return chip
+
+        lax.fori_loop(1, chips + 1, step, b)
         homes[kind][b] = out[2 * b + core]
         send(b, 1 - core)
 

time: 59.1 us -> 57.9 us (0.980)
  Pallas kernels: 58 us -> 56.8 us
    pallas_call x1, Pallas kernels: 58 us -> 56.8 us  [body(): pl.pallas_call(lambda *refs: kernel(chips, *refs), out_shape=pltpu.VMEM((...]
where the time goes in v5:
time: 57.9 us; the launch traced here: 57.8 us
  Pallas kernels  56.8 us (98%)
  local copies, waits for them, and re-layouts  1.04 us (2%)
    pallas_call x1, Pallas kernels, body(): pl.pallas_call(lambda *refs: kernel(chips, *refs), out_shape=pltpu.VMEM((...  56.8 us

profile of v5, /device:TPU:1, one launch (start us, length us, event | category | flops | bytes accessed | tf_op | source)
XLA Modules:
  0.0 57.8 jit_solution(3102614843900962315)
XLA Ops:
  0.0 56.8 %lattice_and_owners.1 = f32[19,32,512]{2,1,0:T(8,128)S(1)} custom-call(f32[19,32,512]{2,1,0:T(8,128)} %bitcast.3, s32[32]{0:T(128)} %refs_1_.1, s32[32]{0:T(128)} %refs_2_.1), custom_call_target="tpu_custom_call" | custom-call | tf_op jit(solution)/shard_map/lattice_and_owners/pallas_call | solution.py:707
  56.8 1.0 %copy.5 = f32[32,19,512]{2,0,1:T(8,128)} copy(f32[32,19,512]{2,0,1:T(8,128)S(1)} %bitcast.2) | data formatting | bytes 2490368

commit v6 on v5

--- a/solution.py
+++ b/solution.py
@@ -606,7 +606,7 @@
                 wide[at(3), :] = chosen([(wide[at(m), :], 3) for m in range(3)])
             return carry
 
-        lax.fori_loop(0, 2 * chips, widen, 0, unroll=8)
+        lax.fori_loop(0, 2 * chips, widen, 0, unroll=32)
 
         def pick(chip, target_core):
             owner = 2 * chip + target_core

time: 57.9 us -> 57.2 us (0.988)
  Pallas kernels: 56.8 us -> 56 us
    pallas_call x1, Pallas kernels: 56.8 us -> 56 us  [body(): pl.pallas_call(lambda *refs: kernel(chips, *refs), out_shape=pltpu.VMEM((...]
where the time goes in v6:
time: 57.2 us; the launch traced here: 57.1 us
  Pallas kernels  56 us (98%)
  local copies, waits for them, and re-layouts  1.04 us (2%)
    pallas_call x1, Pallas kernels, body(): pl.pallas_call(lambda *refs: kernel(chips, *refs), out_shape=pltpu.VMEM((...  56 us

profile of v6, /device:TPU:1, one launch (start us, length us, event | category | flops | bytes accessed | tf_op | source)
XLA Modules:
  0.0 57.1 jit_solution(5537420296158540801)
XLA Ops:
  0.0 56.0 %lattice_and_owners.1 = f32[19,32,512]{2,1,0:T(8,128)S(1)} custom-call(f32[19,32,512]{2,1,0:T(8,128)} %bitcast.3, s32[32]{0:T(128)} %refs_1_.1, s32[32]{0:T(128)} %refs_2_.1), custom_call_target="tpu_custom_call" | custom-call | tf_op jit(solution)/shard_map/lattice_and_owners/pallas_call | solution.py:707
  56.0 1.0 %copy.5 = f32[32,19,512]{2,0,1:T(8,128)} copy(f32[32,19,512]{2,0,1:T(8,128)S(1)} %bitcast.2) | data formatting | bytes 2490368

commit v7 on v6

--- a/solution.py
+++ b/solution.py
@@ -606,7 +606,7 @@
                 wide[at(3), :] = chosen([(wide[at(m), :], 3) for m in range(3)])
             return carry
 
-        lax.fori_loop(0, 2 * chips, widen, 0, unroll=32)
+        lax.fori_loop(0, 2 * chips, widen, 0, unroll=64)
 
         def pick(chip, target_core):
             owner = 2 * chip + target_core

time: 57.2 us -> 57 us (level)
  no operation moved by 1% of the time
where the time goes in v7:
time: 57 us; the launch traced here: 56.9 us
  Pallas kernels  55.9 us (98%)
  local copies, waits for them, and re-layouts  1.04 us (2%)
    pallas_call x1, Pallas kernels, body(): pl.pallas_call(lambda *refs: kernel(chips, *refs), out_shape=pltpu.VMEM((...  55.9 us

profile of v7, /device:TPU:1, one launch (start us, length us, event | category | flops | bytes accessed | tf_op | source)
XLA Modules:
  0.0 56.9 jit_solution(14255817092203973518)
XLA Ops:
  0.0 55.9 %lattice_and_owners.1 = f32[19,32,512]{2,1,0:T(8,128)S(1)} custom-call(f32[19,32,512]{2,1,0:T(8,128)} %bitcast.3, s32[32]{0:T(128)} %refs_1_.1, s32[32]{0:T(128)} %refs_2_.1), custom_call_target="tpu_custom_call" | custom-call | tf_op jit(solution)/shard_map/lattice_and_owners/pallas_call | solution.py:707
  55.9 1.0 %copy.5 = f32[32,19,512]{2,0,1:T(8,128)} copy(f32[32,19,512]{2,0,1:T(8,128)S(1)} %bitcast.2) | data formatting | bytes 2490368
